TPU v7x, 32 devices: a whole 2x2x4 slice. The times are simulated.
32 devices in a mesh: dp: 16 (over z, y, core), tensor: 2 (over x).
Axes of the slice: x: 2, y: 2, z: 4, core: 2. Of those that a mesh axis runs over, the one named last changes fastest.
Arguments:
- step: int32 [1], replicated, may hold values from 0 to 999
- activations: bfloat16 [2, 16384, 8192], P(None, 'dp', 'tensor'), may hold values from -6 to 6
- grad_weight: bfloat16 [2, 8192, 28672], P(None, 'tensor', 'dp'), may hold values from -6 to 6
Outputs:
- preconditioned: float32 [8192, 28672], P('tensor', 'dp')
All inputs are finite; a program needn't handle non-finite values.
Results may differ from a plain program's by a relative error of at most 0.0044.
Values may be sent and summed in bfloat16 or wider, within the bound.
No kernel may reach another device: no remote copies, remote signals or barrier semaphores. Data moves between devices by JAX's collectives and lax.ppermute only.
A program may use at most 192 MiB of HBM per device.

v0:
```python
import jax
import jax.numpy as jnp
from jax import lax
from jax.sharding import PartitionSpec as P

BLOCK = 1024
LAYERS = 2
ITERS = 4


def local(step, activations, grad_weight):
    groups = lax.axis_size("dp")
    layer = step[0] % LAYERS
    damping = 0.05 + 0.1 * step[0].astype(jnp.float32) / 1000.0
    acts = lax.dynamic_index_in_dim(activations, layer, 0, keepdims=False)
    grads = lax.dynamic_index_in_dim(grad_weight, layer, 0, keepdims=False)
    tok_rows = acts.shape[0]
    width = acts.shape[1]
    nblock = width // BLOCK
    share = BLOCK // groups
    blocks = acts.reshape(tok_rows, nblock, BLOCK)
    total_tokens = tok_rows * groups
    first = lax.axis_index("dp") * share
    summed = lax.psum(
        jnp.einsum("tkr,tkc->rkc", blocks, blocks, preferred_element_type=jnp.float32), "dp"
    )
    gram_rows = lax.dynamic_slice_in_dim(summed, first, share, 0)
    row_ids = first + lax.broadcasted_iota(jnp.int32, (share, 1, BLOCK), 0)
    col_ids = lax.broadcasted_iota(jnp.int32, (share, 1, BLOCK), 2)
    identity = (row_ids == col_ids).astype(jnp.float32)
    factor = gram_rows / total_tokens + damping * identity
    block_squares = lax.psum(jnp.sum(factor * factor, axis=(0, 2)), "dp")
    largest = lax.pmax(jnp.max(block_squares), "tensor")
    iterate = jnp.broadcast_to(identity / jnp.sqrt(largest), factor.shape)
    for sweep in range(ITERS):
        whole = lax.all_gather(iterate, "dp", axis=0, tiled=True)
        product = jnp.einsum("rkj,jkc->rkc", factor, whole, precision=lax.Precision.HIGHEST)
        iterate = 2.0 * iterate - jnp.einsum(
            "rkj,jkc->rkc", product, whole, precision=lax.Precision.HIGHEST
        )
    inverse = iterate.astype(jnp.bfloat16)
    stacked = grads.reshape(nblock, BLOCK, grads.shape[1])
    result = jnp.einsum(
        "rkc,kcf->krf",
        lax.all_gather(inverse, "dp", axis=0, tiled=True),
        stacked,
        preferred_element_type=jnp.float32,
    )
    return result.reshape(width, grads.shape[1])


def solution(mesh):
    in_specs = (P(), P(None, "dp", "tensor"), P(None, "tensor", "dp"))
    out_specs = P("tensor", "dp")
    return jax.shard_map(local, mesh=mesh, in_specs=in_specs, out_specs=out_specs, check_vma=False)
```

profile of v0, /device:TPU:0, one launch (start us, length us, event | category | flops | bytes accessed | tf_op | source)
XLA Modules:
  0.0 1019.5 jit_solution(3891566731821359104)
XLA Ops:
  6.5 0.0 all-reduce.2.cloned.1.call-start
  7.2 7.9 constant_dynamic-slice_fusion.1
  15.1 12.0 %copy.23 = bf16[1,1024,4096]{1,2,0:T(8,128)(2,1)} copy(bf16[1,1024,4096]{2,1,0:T(8,128)(2,1)} %constant_dynamic-slice_fusion.1) | data formatting | bytes 16777216
  27.1 17.1 %convolution_bitcast_fusion = f32[1024,4,1024]{2,0,1:T(8,128)} fusion(bf16[1024,4,1024]{0,2,1:T(8,128)(2,1)} %bitcast.51), kind=kOutput, calls=%fused_computation | convolution fusion | flops 8589934592 | bytes 25165824 | tf_op jit(solution)/shard_map/tkr,tkc->rkc/dot_general | solution.py:25
  44.2 0.0 all-reduce.2.cloned.1.call-update
  44.3 0.0 all-gather.14.cloned.1.call-start
  44.3 0.1 fusion.18
  44.4 300.7 %all-reduce.2.cloned.1.call-done = f32[1024,4,1024]{2,0,1:T(8,128)} async-done(((f32[1024,4,1024]{2,0,1:T(8,128)}), f32[1024,4,1024]{2,0,1:T(8,128)}) %all-reduce.2.cloned.1.call-update) | async-done | bytes 16777232 | tf_op jit(solution)/shard_map/psum | solution.py:24
  345.1 1.5 multiply_reduce_fusion
  346.6 31.8 %psum.15 = f32[4]{0:T(128)S(1)} all-reduce(f32[4]{0:T(128)S(1)} %multiply_reduce_fusion), channel_id=1, replica_groups=mesh['dp'=16,'tensor'=2] {'dp'}, use_global_device_ids=true, to_apply=%region_2.3 | all-reduce | flops 4 | bytes 32 | tf_op jit(solution)/shard_map/psum | solution.py:32
  378.4 0.6 reduce_max.9
  379.0 5.5 pmax.7
  385.2 0.8 broadcast_multiply_fusion
  386.0 0.0 all-gather.14.cloned.1.call-update
  386.0 0.3 all-gather.6.cloned.1.call-start
  386.3 47.5 %all-gather.14.cloned.1.call-done = f32[1024,1024]{1,0:T(8,128)} async-done(((f32[64,1024]{1,0:T(8,128)}), f32[1024,1024]{1,0:T(8,128)}) %all-gather.14.cloned.1.call-update) | async-done | bytes 4194320 | tf_op jit(solution)/shard_map/all_gather | solution.py:36
  433.8 11.8 %fusion.4 = f32[64,4,1024]{2,0,1:T(8,128)S(1)} fusion(f32[1024,1024]{1,0:T(8,128)} %all-gather.14.cloned.1.call-done, f32[1024,4,1024]{2,0,1:T(8,128)} %all-reduce.2.cloned.1.call-done, s32[]{:T(128)S(6)} %select_n.18, f32[64,1024]{1,0:T(8,128)S(1)} %fusion.18), kind=kOutput, calls=%fused_computation.5 | convolution fusion | flops 3221749760 | bytes 6553604 | tf_op jit(solution)/shard_map/rkj,jkc->rkc/dot_general | solution.py:37
  445.6 12.8 %fusion.10 = f32[64,4,1024]{2,0,1:T(8,128)} fusion(f32[64,4,1024]{2,0,1:T(8,128)S(1)} %fusion.4, f32[1024,1024]{1,0:T(8,128)} %all-gather.14.cloned.1.call-done, f32[64,1024]{1,0:T(8,128)S(1)} %get-tuple-element.5), kind=kOutput, calls=%fused_computation.7 | convolution fusion | flops 3221487616 | bytes 6553600 | tf_op jit(solution)/shard_map/rkj,jkc->rkc/dot_general | solution.py:38
  458.3 0.0 copy-start.4
  458.3 0.0 all-gather.6.cloned.1.call-update
  458.4 0.0 all-gather.8.cloned.1.call-start
  458.4 125.1 %all-gather.6.cloned.1.call-done = f32[1024,4,1024]{2,0,1:T(8,128)} async-done(((f32[64,4,1024]{2,0,1:T(8,128)}), f32[1024,4,1024]{2,0,1:T(8,128)}) %all-gather.6.cloned.1.call-update) | async-done | bytes 16777232 | tf_op jit(solution)/shard_map/all_gather | solution.py:36
  583.5 0.0 copy-start.1
  583.5 15.3 %convolution_bitcast_fusion.6 = f32[64,4,1024]{2,0,1:T(8,128)S(1)} fusion(f32[1024,4,1024]{2,0,1:T(8,128)} %all-gather.6.cloned.1.call-done, f32[1024,4,1024]{2,0,1:T(8,128)} %all-reduce.2.cloned.1.call-done, s32[]{:T(128)S(6)} %select_n.18, f32[64,1024]{1,0:T(8,128)S(1)} %fusion.18), kind=kOutput, calls=%fused_computation.16 | convolution fusion | flops 3221749760 | bytes 19136516 | tf_op jit(solution)/shard_map/rkj,jkc->rkc/dot_general | solution.py:37
  598.8 0.0 copy-done.4
  598.8 0.0 copy-done.1
  598.8 11.8 %fusion.15 = f32[64,4,1024]{2,0,1:T(8,128)} fusion(f32[1024,4,1024]{2,0,1:T(8,128)S(1)} %copy-done.1, f32[64,4,1024]{2,0,1:T(8,128)S(1)} %convolution_bitcast_fusion.6, f32[64,4,1024]{2,0,1:T(8,128)S(1)} %copy-done.4), kind=kOutput, calls=%fused_computation.15 | convolution fusion | flops 3221749760 | bytes 19922944 | tf_op jit(solution)/shard_map/rkj,jkc->rkc/dot_general | solution.py:38
  610.6 0.0 copy-start.5
  610.6 0.0 all-gather.8.cloned.1.call-update
  610.6 0.0 all-gather.10.cloned.1.call-start
  610.7 124.7 %all-gather.8.cloned.1.call-done = f32[1024,4,1024]{2,0,1:T(8,128)} async-done(((f32[64,4,1024]{2,0,1:T(8,128)}), f32[1024,4,1024]{2,0,1:T(8,128)}) %all-gather.8.cloned.1.call-update) | async-done | bytes 16777232 | tf_op jit(solution)/shard_map/all_gather | solution.py:36
  735.4 0.0 copy-start.2
  735.4 15.0 %convolution_bitcast_fusion.4 = f32[64,4,1024]{2,0,1:T(8,128)S(1)} fusion(f32[1024,4,1024]{2,0,1:T(8,128)} %all-gather.8.cloned.1.call-done, f32[1024,4,1024]{2,0,1:T(8,128)} %all-reduce.2.cloned.1.call-done, s32[]{:T(128)S(6)} %select_n.18, f32[64,1024]{1,0:T(8,128)S(1)} %fusion.18), kind=kOutput, calls=%fused_computation.13 | convolution fusion | flops 3221749760 | bytes 19136516 | tf_op jit(solution)/shard_map/rkj,jkc->rkc/dot_general | solution.py:37
  750.4 0.0 copy-done.5
  750.4 0.0 copy-done.2
  750.4 11.8 %fusion.14 = f32[64,4,1024]{2,0,1:T(8,128)} fusion(f32[1024,4,1024]{2,0,1:T(8,128)S(1)} %copy-done.2, f32[64,4,1024]{2,0,1:T(8,128)S(1)} %convolution_bitcast_fusion.4, f32[64,4,1024]{2,0,1:T(8,128)S(1)} %copy-done.5), kind=kOutput, calls=%fused_computation.12 | convolution fusion | flops 3221749760 | bytes 19922944 | tf_op jit(solution)/shard_map/rkj,jkc->rkc/dot_general | solution.py:38
  762.2 0.0 copy-start.3
  762.2 0.0 all-gather.10.cloned.1.call-update
  762.2 0.0 all-gather.12.cloned.1.call-start
  762.3 124.7 %all-gather.10.cloned.1.call-done = f32[1024,4,1024]{2,0,1:T(8,128)} async-done(((f32[64,4,1024]{2,0,1:T(8,128)}), f32[1024,4,1024]{2,0,1:T(8,128)}) %all-gather.10.cloned.1.call-update) | async-done | bytes 16777232 | tf_op jit(solution)/shard_map/all_gather | solution.py:36
  887.0 15.0 %convolution_bitcast_fusion.2 = f32[64,4,1024]{2,0,1:T(8,128)S(1)} fusion(f32[1024,4,1024]{2,0,1:T(8,128)} %all-gather.10.cloned.1.call-done, f32[1024,4,1024]{2,0,1:T(8,128)} %all-reduce.2.cloned.1.call-done, s32[]{:T(128)S(6)} %select_n.18, f32[64,1024]{1,0:T(8,128)S(1)} %fusion.18), kind=kOutput, calls=%fused_computation.10 | convolution fusion | flops 3221749760 | bytes 19136516 | tf_op jit(solution)/shard_map/rkj,jkc->rkc/dot_general | solution.py:37
  902.0 0.0 copy-done.3
  902.0 0.0 copy-done
  902.0 11.6 %fusion.16 = bf16[64,4,1024]{2,0,1:T(8,128)(2,1)} fusion(f32[1024,4,1024]{2,0,1:T(8,128)S(1)} %copy-done, f32[64,4,1024]{2,0,1:T(8,128)S(1)} %convolution_bitcast_fusion.2, f32[64,4,1024]{2,0,1:T(8,128)S(1)} %copy-done.3), kind=kOutput, calls=%fused_computation.17 | convolution fusion | flops 3222011904 | bytes 19398656 | tf_op jit(solution)/shard_map/rkj,jkc->rkc/dot_general | solution.py:38
  913.7 0.0 all-gather.12.cloned.1.call-update
  913.7 13.2 %constant_dynamic-slice_fusion = bf16[1,4096,1792]{2,1,0:T(8,128)(2,1)} fusion(bf16[2,4096,1792]{2,1,0:T(8,128)(2,1)} %param.5, s32[]{:T(128)S(6)} %select_n.17), kind=kLoop, calls=%fused_computation.24 | loop fusion | bytes 29360132 | tf_op jit(solution)/shard_map/jit(dynamic_index_in_dim)/dynamic_slice | solution.py:16
  926.9 59.4 %all-gather.12.cloned.1.call-done = bf16[1024,4,1024]{2,0,1:T(8,128)(2,1)} async-done(((bf16[64,4,1024]{2,0,1:T(8,128)(2,1)}), bf16[1024,4,1024]{2,0,1:T(8,128)(2,1)}) %all-gather.12.cloned.1.call-update) | async-done | bytes 8388624 | tf_op jit(solution)/shard_map/all_gather | solution.py:45
  986.3 25.9 %fusion.19 = f32[4,1024,1792]{2,1,0:T(8,128)} fusion(bf16[1024,4,1024]{2,0,1:T(8,128)(2,1)} %all-gather.12.cloned.1.call-done, bf16[4,1024,1792]{2,1,0:T(8,128)(2,1)} %bitcast.50), kind=kOutput, calls=%fused_computation.27 | convolution fusion | flops 15032385536 | bytes 52428800 | tf_op jit(solution)/shard_map/rkc,kcf->krf/dot_general | solution.py:43
  (2 shorter events, 0.0 us)
Async XLA Ops:
  6.5 338.6 %all-reduce.2.cloned.1.call-start = ((), (), s32[]{:S(2)}) async-start(), calls=%async_computation | async-start | bytes 33554432 | tf_op jit(solution)/shard_map/psum | solution.py:24
  44.3 389.5 %all-gather.14.cloned.1.call-start = ((), (), s32[]{:S(2)}) async-start(), calls=%async_computation.5 | async-start | bytes 4456448 | tf_op jit(solution)/shard_map/all_gather | solution.py:36
  386.0 197.5 %all-gather.6.cloned.1.call-start = ((), (), s32[]{:S(2)}) async-start(), calls=%async_computation.1 | async-start | bytes 17825792 | tf_op jit(solution)/shard_map/all_gather | solution.py:36
  458.3 140.4 %copy-start.4 = (f32[64,4,1024]{2,0,1:T(8,128)S(1)}, f32[64,4,1024]{2,0,1:T(8,128)}, u32[]{:S(2)}) copy-start(f32[64,4,1024]{2,0,1:T(8,128)} %fusion.10) | copy-start | bytes 3145732
  458.4 277.0 %all-gather.8.cloned.1.call-start = ((), (), s32[]{:S(2)}) async-start(), calls=%async_computation.2 | async-start | bytes 17825792 | tf_op jit(solution)/shard_map/all_gather | solution.py:36
  583.5 15.3 %copy-start.1 = (f32[1024,4,1024]{2,0,1:T(8,128)S(1)}, f32[1024,4,1024]{2,0,1:T(8,128)}, u32[]{:S(2)}) copy-start(f32[1024,4,1024]{2,0,1:T(8,128)} %all-gather.6.cloned.1.call-done) | copy-start | bytes 50331652
  610.6 139.8 %copy-start.5 = (f32[64,4,1024]{2,0,1:T(8,128)S(1)}, f32[64,4,1024]{2,0,1:T(8,128)}, u32[]{:S(2)}) copy-start(f32[64,4,1024]{2,0,1:T(8,128)} %fusion.15) | copy-start | bytes 3145732
  610.6 276.4 %all-gather.10.cloned.1.call-start = ((), (), s32[]{:S(2)}) async-start(), calls=%async_computation.3 | async-start | bytes 17825792 | tf_op jit(solution)/shard_map/all_gather | solution.py:36
  735.4 15.0 %copy-start.2 = (f32[1024,4,1024]{2,0,1:T(8,128)S(1)}, f32[1024,4,1024]{2,0,1:T(8,128)}, u32[]{:S(2)}) copy-start(f32[1024,4,1024]{2,0,1:T(8,128)} %all-gather.8.cloned.1.call-done) | copy-start | bytes 50331652
  762.2 139.8 %copy-start.3 = (f32[64,4,1024]{2,0,1:T(8,128)S(1)}, f32[64,4,1024]{2,0,1:T(8,128)}, u32[]{:S(2)}) copy-start(f32[64,4,1024]{2,0,1:T(8,128)} %fusion.14) | copy-start | bytes 3145732
  762.2 224.1 %all-gather.12.cloned.1.call-start = ((), (), s32[]{:S(2)}) async-start(), calls=%async_computation.4 | async-start | bytes 8912896 | tf_op jit(solution)/shard_map/all_gather | solution.py:45
  887.0 15.0 %copy-start = (f32[1024,4,1024]{2,0,1:T(8,128)S(1)}, f32[1024,4,1024]{2,0,1:T(8,128)}, u32[]{:S(2)}) copy-start(f32[1024,4,1024]{2,0,1:T(8,128)} %all-gather.10.cloned.1.call-done) | copy-start | bytes 50331652
Sparse Core Ops, SparseCore 0:
  44.4 300.6 all-reduce.1
  386.1 47.5 all-gather.13
  458.5 124.9 all-gather.5
  610.7 124.6 all-gather.7
  762.3 124.6 all-gather.9
  913.8 72.4 all-gather.11
where the time goes:
time: 1020 us
  waiting for transfers between devices  782 us (77%)
  matrix products  148 us (15%)
  blocking collectives  37.3 us (4%)
  local copies, waits for them, and re-layouts  33.2 us (3%)
  between operations  15.4 us (2%)
    all_gather x4, waiting for transfers between devices, local(): whole = lax.all_gather(iterate, 'dp', axis=0, tiled=True)  422 us
    psum x1, waiting for transfers between devices, local(): lax.psum(jnp.einsum('tkr,tkc->rkc', blocks, blocks, preferred_element_typ...  301 us
    all_gather x1, waiting for transfers between devices, local(): lax.all_gather(inverse, 'dp', axis=0, tiled=True)  59.4 us
    dot_general x4, matrix products, local(): jnp.einsum('rkj,jkc->rkc', factor, whole, precision=lax.Precision.HIGHEST)  57 us
    dot_general x4, matrix products, local(): jnp.einsum('rkj,jkc->rkc', product, whole, precision=lax.Precision.HIGHEST)  48 us
    psum x1, blocking collectives, local(): block_squares = lax.psum(jnp.sum(factor * factor, axis=(0, 2)), 'dp')  31.8 us
    dot_general x1, matrix products, local(): jnp.einsum('rkc,kcf->krf', lax.all_gather(inverse, 'dp', axis=0, tiled=Tr...  25.9 us
  transfers between devices with their start and end apart: 6, of which 6 were waited for; matrix products, arithmetic and copies ran while one was open for 1% of the time, Pallas kernels for 0%

commit v1 on v0

v1 whole, which is shorter than its diff:
```python
import jax
import jax.numpy as jnp
from jax import lax
from jax.experimental import pallas as pl
from jax.experimental.pallas import tpu as pltpu
from jax.sharding import PartitionSpec as P


BLOCK = 1024
LAYERS = 2
TILE = 256
HALF = TILE // 2
NT = BLOCK // TILE
OFF = [(i, j) for i in range(NT) for j in range(i + 1, NT)]
SLOTS = len(OFF) + NT - 1
ROWS = SLOTS * TILE
QUARTS = ((0, 0), (0, HALF), (HALF, HALF))
DIAG0 = len(OFF)
LIMIT = 60 * 1024 * 1024


def pack(dst, tile_of):
    for s, (i, j) in enumerate(OFF):
        dst[s * TILE:(s + 1) * TILE, :] = tile_of(i, j).astype(dst.dtype)
    last = tile_of(NT - 1, NT - 1).astype(dst.dtype)
    for d in range(NT - 1):
        r = (DIAG0 + d) * TILE
        t = tile_of(d, d).astype(dst.dtype)
        dst[r:r + HALF, :] = t[:HALF, :]
        dst[r + HALF:r + TILE, HALF:] = t[HALF:, HALF:]
        y, x = QUARTS[d]
        dst[r + HALF:r + TILE, :HALF] = last[y:y + HALF, x:x + HALF]


def unpack(src, put, dtype):
    for s, (i, j) in enumerate(OFF):
        t = src[s * TILE:(s + 1) * TILE, :].astype(dtype)
        put(i * TILE, j * TILE, t)
        put(j * TILE, i * TILE, t.T)
    for d in range(NT - 1):
        r = (DIAG0 + d) * TILE
        o = d * TILE
        upper = src[r:r + HALF, HALF:].astype(dtype)
        put(o, o, src[r:r + HALF, :HALF].astype(dtype))
        put(o, o + HALF, upper)
        put(o + HALF, o, upper.T)
        put(o + HALF, o + HALF, src[r + HALF:r + TILE, HALF:].astype(dtype))
        y, x = QUARTS[d]
        e = (NT - 1) * TILE
        part = src[r + HALF:r + TILE, :HALF].astype(dtype)
        put(e + y, e + x, part)
        if x != y:
            put(e + x, e + y, part.T)


def dot(a, b, dims=((1,), (0,))):
    return lax.dot_general(a, b, (dims, ((), ())), preferred_element_type=jnp.float32)


def gram_body(info, acts, keep, send, scratch):
    for i in range(NT):
        panel = dot(acts[:, i * TILE:(i + 1) * TILE], acts[:, i * TILE:], ((0,), (0,)))
        for s, (a, b) in enumerate(OFF):
            if a == i:
                o = (b - i) * TILE
                scratch[s * TILE:(s + 1) * TILE, :] = panel[:, o:o + TILE].astype(scratch.dtype)
        t = panel[:, :TILE].astype(scratch.dtype)
        if i < NT - 1:
            r = (DIAG0 + i) * TILE
            scratch[r:r + HALF, :] = t[:HALF, :]
            scratch[r + HALF:r + TILE, HALF:] = t[HALF:, HALF:]
        else:
            for d, (y, x) in enumerate(QUARTS):
                r = (DIAG0 + d) * TILE
                scratch[r + HALF:r + TILE, :HALF] = t[y:y + HALF, x:x + HALF]
    if send is None:
        keep[...] = scratch[...]
    else:
        rows = ROWS // 2
        core = info[1]
        keep[...] = scratch[pl.ds(pl.multiple_of(core * rows, HALF), rows), :]
        send[...] = scratch[pl.ds(pl.multiple_of((1 - core) * rows, HALF), rows), :]


def gram(info, activations, nblock, split):
    tok = activations.shape[1]
    rows = ROWS // 2 if split else ROWS
    spec = pl.BlockSpec((None, rows, TILE), lambda b, info: (b, 0, 0))
    shape = jax.ShapeDtypeStruct((nblock, rows, TILE), jnp.bfloat16)

    def body(info, acts, *rest):
        if split:
            gram_body(info, acts, *rest)
        else:
            gram_body(info, acts, rest[0], None, rest[1])

    return pl.pallas_call(
        body,
        grid_spec=pltpu.PrefetchScalarGridSpec(
            num_scalar_prefetch=1,
            grid=(nblock,),
            in_specs=[pl.BlockSpec((None, tok, BLOCK), lambda b, info: (info[0], 0, b))],
            out_specs=[spec, spec] if split else [spec],
            scratch_shapes=[pltpu.VMEM((ROWS, TILE), jnp.bfloat16)],
        ),
        out_shape=[shape, shape] if split else [shape],
        compiler_params=pltpu.CompilerParams(vmem_limit_bytes=LIMIT),
        name="gram",
    )(info, activations)


def squares(packed, damping, tokens):
    f = packed.astype(jnp.float32)
    r = lax.broadcasted_iota(jnp.int32, (ROWS, TILE), 0)
    c = lax.broadcasted_iota(jnp.int32, (ROWS, TILE), 1)
    slot = r // TILE - DIAG0
    rr = r % TILE
    low = (rr >= HALF) & (c < HALF)
    on = ((low & (rr - HALF == c) & (slot != 1)) | (rr == c)) & (slot >= 0)
    twice = (slot < 0) | (low & (slot == 1)) | ((rr < HALF) & (c >= HALF))
    f = f / tokens + jnp.where(on, damping, 0.0)
    return jnp.sum(f * f * jnp.where(twice, 2.0, 1.0))


def factor_into(damp, packed, f, fb, tokens):
    damping = damp[0]
    inv = 1.0 / tokens

    def put(r, c, v):
        h, w = v.shape
        v = v * inv
        if r == c:
            eye = (lax.broadcasted_iota(jnp.int32, v.shape, 0)
                   == lax.broadcasted_iota(jnp.int32, v.shape, 1))
            v = v + jnp.where(eye, damping, 0.0)
        if f is not None:
            f[r:r + h, c:c + w] = v
        if fb is not None:
            fb[r:r + h, c:c + w] = v.astype(jnp.bfloat16)

    unpack(packed, put, jnp.float32)


STRIPS = [slice(i * TILE, (i + 1) * TILE) for i in range(NT)]


VM = pl.BlockSpec(memory_space=pltpu.VMEM)
SM = pl.BlockSpec(memory_space=pltpu.SMEM)
THIN = jax.ShapeDtypeStruct((BLOCK, BLOCK), jnp.bfloat16)
PARAMS = pltpu.CompilerParams(vmem_limit_bytes=LIMIT)


ANY = pl.BlockSpec(memory_space=pl.ANY)
VFULL = pltpu.VMEM((BLOCK, BLOCK), jnp.float32)
VTHIN = pltpu.VMEM((BLOCK, BLOCK), jnp.bfloat16)


def powers_body(damp, packed, h2, h3, fb, p2, p3, sems, *, tokens):
    factor_into(damp, packed, None, fb, tokens)
    for r in STRIPS:
        p2[r, :] = dot(fb[r, :], fb[...]).astype(p2.dtype)
    first = pltpu.make_async_copy(p2, h2, sems.at[0])
    first.start()
    for r in STRIPS:
        p3[r, :] = dot(p2[r, :], fb[...]).astype(p3.dtype)
    second = pltpu.make_async_copy(p3, h3, sems.at[1])
    second.start()
    first.wait()
    second.wait()


def powers(damping, packed, tokens):
    return pl.pallas_call(
        lambda *refs: powers_body(*refs, tokens=tokens),
        in_specs=[SM, VM],
        out_specs=[ANY, ANY],
        out_shape=[THIN, THIN],
        scratch_shapes=[VTHIN, VTHIN, VTHIN, pltpu.SemaphoreType.DMA((2,))],
        compiler_params=PARAMS,
        cost_estimate=pl.CostEstimate(
            flops=4 * BLOCK**3, transcendentals=0, bytes_accessed=BLOCK * BLOCK * 6
        ),
        name="powers",
    )(damping, packed)


def finish_body(info, damp, top, packed, h2, h3, out, piece, f, p2, p3, e, h, k, eb, kb, sems, *, tokens):
    loads = [pltpu.make_async_copy(a, b, sems.at[i]) for i, (a, b) in enumerate(((h2, p2), (h3, p3)))]
    for load in loads:
        load.start()
    factor_into(damp, packed, f, None, tokens)
    c = 1.0 / jnp.sqrt(jnp.max(top[...], axis=(0, 1), keepdims=True))
    for load in loads:
        load.wait()
    for r in STRIPS:
        cf = c * f[r, :]
        q2 = (c * c) * p2[r, :].astype(jnp.float32)
        q3 = (c * c * c) * p3[r, :].astype(jnp.float32)
        v = 3.0 * (cf - q2) + q3
        e[r, :] = v
        eb[r, :] = v.astype(jnp.bfloat16)
        f[r, :] = 6.0 * cf - 4.0 * q2 + q3
    for r in STRIPS:
        hv = 2.0 * e[r, :] - dot(eb[r, :], eb[...])
        h[r, :] = hv
        w = hv + 0.5 * e[r, :]
        kb[r, :] = w.astype(jnp.bfloat16)
    for r in STRIPS:
        k[r, :] = 3.75 * h[r, :] + 2.5 * e[r, :] - dot(kb[r, :], kb[...])
    for r in STRIPS:
        kb[r, :] = k[r, :].astype(jnp.bfloat16)
    for i, r in enumerate(STRIPS):
        cols = slice(i * TILE, BLOCK)
        x = dot(f[r, :].astype(jnp.bfloat16), kb[:, cols]) - 3.0 * k[r, cols] - 5.0 * f[r, cols]
        eye = (lax.broadcasted_iota(jnp.int32, x.shape, 0)
               == lax.broadcasted_iota(jnp.int32, x.shape, 1))
        e[r, cols] = c * (x + jnp.where(eye, 16.0, 0.0))
    pack(out, lambda i, j: e[i * TILE:(i + 1) * TILE, j * TILE:(j + 1) * TILE])
    n = piece.shape[0]
    piece[...] = out[pl.ds(pl.multiple_of(info[8] * n, HALF // 2), n), :]


def finish(info, damping, top, packed, p2, p3, tokens):
    return pl.pallas_call(
        lambda *refs: finish_body(*refs, tokens=tokens),
        in_specs=[SM, SM, VM, VM, ANY, ANY],
        out_specs=[VM, VM],
        out_shape=[
            jax.ShapeDtypeStruct((ROWS, TILE), jnp.bfloat16),
            jax.ShapeDtypeStruct((ROWS // 4, TILE), jnp.bfloat16),
        ],
        scratch_shapes=[VFULL, VTHIN, VTHIN, VFULL, VFULL, VFULL, VTHIN, VTHIN,
                        pltpu.SemaphoreType.DMA((2,))],
        compiler_params=PARAMS,
        name="finish",
    )(info, damping, top, packed, p2, p3)


CHUNK = 512
DEPTH = 3


def apply_body(info, *refs, count, blocks, first, aliased, cols):
    npiece = count * len(blocks)
    pieces = refs[:npiece]
    grads = refs[npiece]
    out, packed, x, g, o, psem, gsem, osem = refs[npiece + 1 + aliased:]
    n = ROWS // count
    chunks = [(c, min(CHUNK, cols - c)) for c in range(0, cols, CHUNK)]
    steps = [(b, c, w) for b in range(len(blocks)) for c, w in chunks]

    def rows(b):
        return pl.ds(pl.multiple_of(info[blocks[b]] * BLOCK, BLOCK), BLOCK)

    def load(s):
        b, c, w = steps[s]
        return pltpu.make_async_copy(
            grads.at[info[0], rows(b), pl.ds(c, w)], g.at[s % DEPTH, :, pl.ds(0, w)], gsem.at[s % DEPTH])

    def store(s):
        b, c, w = steps[s]
        return pltpu.make_async_copy(
            o.at[s % DEPTH, :, pl.ds(0, w)], out.at[rows(b), pl.ds(c, w)], osem.at[s % DEPTH])

    def fetch(b, p):
        start = pl.multiple_of(info[first + p] * n, HALF // 2)
        return pltpu.make_async_copy(
            pieces[b * count + p], packed.at[b, pl.ds(start, n), :], psem.at[b * count + p])

    for b in range(len(blocks)):
        for p in range(count):
            fetch(b, p).start()
    for s in range(min(DEPTH, len(steps))):
        load(s).start()
    for s, (b, c, w) in enumerate(steps):
        if c == 0:
            for p in range(count):
                fetch(b, p).wait()

            def put(r, col, v):
                x[b % 2, r:r + v.shape[0], col:col + v.shape[1]] = v

            unpack(packed.at[b], put, x.dtype)
        load(s).wait()
        if s >= DEPTH:
            store(s - DEPTH).wait()
        for r in STRIPS:
            o[s % DEPTH, r, :w] = dot(x[b % 2, r, :], g[s % DEPTH, :, :w])
        store(s).start()
        if s + DEPTH < len(steps):
            load(s + DEPTH).start()
    for s in range(max(0, len(steps) - DEPTH), len(steps)):
        store(s).wait()


def apply_blocks(info, blocks, first, pieces, grad_weight, result):
    width, cols = grad_weight.shape[1:]
    count = len(pieces) // len(blocks)
    aliased = result is not None
    return pl.pallas_call(
        lambda *refs: apply_body(
            *refs, count=count, blocks=blocks, first=first, aliased=int(aliased), cols=cols),
        in_specs=[SM] + [ANY] * (len(pieces) + 1 + int(aliased)),
        out_specs=ANY,
        scratch_shapes=[
            pltpu.VMEM((len(blocks), ROWS, TILE), jnp.bfloat16),
            pltpu.VMEM((2, BLOCK, BLOCK), jnp.bfloat16),
            pltpu.VMEM((DEPTH, BLOCK, CHUNK), jnp.bfloat16),
            pltpu.VMEM((DEPTH, BLOCK, CHUNK), jnp.float32),
            pltpu.SemaphoreType.DMA((len(pieces),)),
            pltpu.SemaphoreType.DMA((DEPTH,)),
            pltpu.SemaphoreType.DMA((DEPTH,)),
        ],
        out_shape=jax.ShapeDtypeStruct((width, cols), jnp.float32),
        input_output_aliases={len(pieces) + 2: 0} if aliased else {},
        compiler_params=PARAMS,
        cost_estimate=pl.CostEstimate(
            flops=2 * BLOCK * BLOCK * cols * len(blocks),
            transcendentals=0,
            bytes_accessed=6 * BLOCK * cols * len(blocks),
        ),
        name="apply",
    )(info, *pieces, grad_weight, *([result] if aliased else []))


def local_any(step, activations, grad_weight):
    groups = lax.axis_size("dp")
    layer = step[0] % LAYERS
    damping = 0.05 + 0.1 * step[0].astype(jnp.float32) / 1000.0
    tokens = activations.shape[1] * groups
    nblock = activations.shape[2] // BLOCK
    damping = damping.reshape(1)
    info = jnp.stack([layer, *[0] * 12, *range(nblock)]).astype(jnp.int32)
    (part,) = gram(info, activations, nblock, False)
    summed = lax.psum(part.astype(jnp.float32), "dp")
    each = jnp.stack([squares(summed[b], damping[0], tokens) for b in range(nblock)])
    top = jnp.broadcast_to(lax.pmax(jnp.max(each), "tensor"), (8, 128))
    result = None
    for b in range(nblock):
        p2, p3 = powers(damping, summed[b], tokens)
        inverse, _ = finish(info, damping, top, summed[b], p2, p3, tokens)
        result = apply_blocks(info, [13 + b], 12, [inverse], grad_weight, result)
    return result


def assemble_body(info, damp, *refs, count, tokens, first):
    pieces = refs[:count]
    out, total = refs[count:]
    n = ROWS // count
    for p, piece in enumerate(pieces):
        start = pl.multiple_of(info[first + p] * n, 64)
        out[pl.ds(start, n), :] = piece[...]
    total[...] = jnp.full(total.shape, squares(out[...], damp[0], tokens), jnp.float32)


def assemble(info, first, damping, pieces, tokens):
    return pl.pallas_call(
        lambda *refs: assemble_body(*refs, count=len(pieces), tokens=tokens, first=first),
        in_specs=[SM, SM] + [VM] * len(pieces),
        out_specs=[VM, VM],
        out_shape=[
            jax.ShapeDtypeStruct((ROWS, TILE), jnp.bfloat16),
            jax.ShapeDtypeStruct((8, 128), jnp.float32),
        ],
        compiler_params=PARAMS,
        name="assemble",
    )(info, damping, *pieces)


def local_quad(step, activations, grad_weight):
    groups = lax.axis_size("dp")
    halves = lax.axis_size("tensor")
    layer = step[0] % LAYERS
    damping = 0.05 + 0.1 * step[0].astype(jnp.float32) / 1000.0
    tokens = activations.shape[1] * groups
    nblock = groups // 4
    me = lax.axis_index("dp")
    z, y, c = me // 4, (me // 2) % 2, me % 2
    f32 = jnp.float32
    bf = jnp.bfloat16

    def move(v, f):
        return lax.ppermute(v, "dp", [(i, f(i)) for i in range(groups)])

    def swap_c(v):
        return move(v, lambda i: i ^ 1)

    def swap_y(v):
        return move(v, lambda i: i ^ 2)

    def shift(v, k):
        return move(v, lambda i: (i + 4 * k) % groups)

    def plus(a, b):
        return (a.astype(f32) + b.astype(f32)).astype(bf)

    def scatter(v):
        parts = [lax.dynamic_index_in_dim(v, z, 0, False).astype(f32)]
        for k in range(1, nblock):
            part = lax.dynamic_index_in_dim(v, (z + k) % nblock, 0, False)
            parts.append(shift(part, k).astype(f32))
        total = parts[0]
        for p in parts[1:]:
            total = total + p
        return total.astype(bf)

    places = [3 * c + y, 3 * c + 1 - y, 3 * c + 2]
    places += [3 * (1 - c) + y, 3 * (1 - c) + 1 - y, 3 * (1 - c) + 2]
    spread = [2 * c + y, 2 * c + 1 - y, 2 * (1 - c) + y, 2 * (1 - c) + 1 - y]
    blocks = [(z - k) % nblock for k in range(nblock)]
    info = jnp.stack([layer, c, *places, *spread, 0, *blocks]).astype(jnp.int32)
    keep, send = gram(info, activations, nblock, True)
    got = swap_c(send)
    third = ROWS // 6

    def rows_of(v, start):
        return lax.dynamic_slice_in_dim(v, start, third, 1)

    early = 2 * third
    zpart = plus(keep[:, early:], got[:, early:])
    other = (1 - y) * third
    mine = y * third
    ysend = plus(rows_of(keep, other), rows_of(got, other))
    ygot = swap_y(ysend)
    zsum = scatter(zpart)
    ypart = (rows_of(keep, mine).astype(f32) + rows_of(got, mine).astype(f32) + ygot.astype(f32)).astype(bf)
    zfull = plus(zsum, swap_y(zsum))
    ysum = scatter(ypart)
    yother = swap_y(ysum)
    own = [ysum, yother, zfull]
    theirs = [swap_c(v) for v in own]
    damping = damping.reshape(1)
    packed, top = assemble(info, 2, damping, own + theirs, tokens)

    d = 1
    while d < nblock:
        moved = move(top, lambda i: i ^ (4 * d))
        top = jnp.maximum(top, moved)
        d *= 2
    d = 1
    while d < halves:
        top = jnp.maximum(top, lax.ppermute(top, "tensor", [(i, i ^ d) for i in range(halves)]))
        d *= 2
    p2, p3 = powers(damping, packed, tokens)
    inverse, piece = finish(info, damping, top, packed, p2, p3, tokens)

    arrived = []
    for k in range(1, nblock):
        arrived.append(shift(piece, k))
    result = apply_blocks(info, [13], 12, [inverse], grad_weight, None)
    pieces = []
    for a in arrived:
        ya = swap_y(a)
        pieces += [a, ya, swap_c(a), swap_c(ya)]
    return apply_blocks(info, [13 + k for k in range(1, nblock)], 8, pieces, grad_weight, result)


def power_of_two(n):
    return n & (n - 1) == 0


def solution(mesh):
    groups, halves = mesh.shape["dp"], mesh.shape["tensor"]

    def local(step, activations, grad_weight):
        nblock = activations.shape[2] // BLOCK
        quad = groups == 4 * nblock and nblock > 1 and power_of_two(groups) and power_of_two(halves)
        return (local_quad if quad else local_any)(step, activations, grad_weight)

    in_specs = (P(), P(None, "dp", "tensor"), P(None, "tensor", "dp"))
    out_specs = P("tensor", "dp")
    return jax.shard_map(local, mesh=mesh, in_specs=in_specs, out_specs=out_specs, check_vma=False)
```

time: 1020 us -> 177 us (0.17)
  the two profiles are of different devices: /device:TPU:0 before, /device:TPU:9 now
where the time goes in v1:
time: 177 us; the launch traced here: 176 us
  Pallas kernels  58.9 us (33%)
  waiting for transfers between devices  54.2 us (31%)
  starting transfers between devices  52.9 us (30%)
  other arithmetic  5.85 us (3%)
  local copies, waits for them, and re-layouts  3.17 us (2%)
    ppermute x27, waiting for transfers between devices, move(): return lax.ppermute(v, 'dp', [(i, f(i)) for i in range(groups)])  54.2 us
    ppermute x27, starting transfers between devices, move(): return lax.ppermute(v, 'dp', [(i, f(i)) for i in range(groups)])  51.7 us
    pallas_call x2, Pallas kernels, apply_blocks(): pl.pallas_call(lambda *refs: apply_body(*refs, count=count, blocks=blocks...  26.6 us
    pallas_call x1, Pallas kernels, finish(): pl.pallas_call(lambda *refs: finish_body(*refs, tokens=tokens), in_specs=...  12 us
    pallas_call x1, Pallas kernels, gram(): pl.pallas_call(body, grid_spec=pltpu.PrefetchScalarGridSpec(num_scalar_pr...  10.2 us
    pallas_call x1, Pallas kernels, powers(): pl.pallas_call(lambda *refs: powers_body(*refs, tokens=tokens), in_specs=...  7.32 us
  transfers between devices with their start and end apart: 28, of which 13 were waited for; matrix products, arithmetic and copies ran while one was open for 1% of the time, Pallas kernels for 9%

profile of v1, /device:TPU:9, one launch (start us, length us, event | category | flops | bytes accessed | tf_op | source)
XLA Modules:
  0.0 176.2 jit_solution(10757230282694140727)
XLA Ops:
  0.7 0.7 stack.67.info.refs_0_
  1.4 10.2 %gram.1 = (bf16[4,1152,256]{2,1,0:T(8,128)(2,1)}, bf16[4,1152,256]{2,1,0:T(8,128)(2,1)}) custom-call(s32[17]{0:T(128)} %stack.67.info.refs_0_, bf16[2,1024,4096]{2,1,0:T(8,128)(2,1)} %acts.1), custom_call_target="tpu_custom_call" | custom-call | tf_op jit(solution)/shard_map/gram/pallas_call | solution.py:97
  11.6 0.7 collective-permute-start
  12.3 4.4 %collective-permute-done = bf16[4,1152,256]{2,1,0:T(8,128)(2,1)S(1)} collective-permute-done((bf16[4,1152,256]{2,1,0:T(8,128)(2,1)}, bf16[4,1152,256]{2,1,0:T(8,128)(2,1)S(1)}, u32[]{:S(2)}, u32[]{:S(2)}) %collective-permute-start) | collective-permute-done | bytes 2359328 | tf_op jit(solution)/shard_map/ppermute | solution.py:383
  16.7 2.7 %add_convert_fusion = (bf16[4,384,256]{2,1,0:T(8,128)(2,1)S(1)}, bf16[4,384,256]{2,1,0:T(8,128)(2,1)}) fusion(bf16[4,1152,256]{2,1,0:T(8,128)(2,1)S(1)} %collective-permute-done, bf16[4,1152,256]{2,1,0:T(8,128)(2,1)} %get-tuple-element.13, s32[]{:T(128)S(6)} %select_n.91), kind=kLoop, calls=%fused_computation | loop fusion | flops 3145728 | bytes 4718596 | tf_op jit(solution)/shard_map/convert_element_type | solution.py:395
  19.3 1.2 collective-permute-start.1
  20.6 1.4 collective-permute-start.6
  22.1 2.3 %collective-permute-start.7 = (bf16[384,256]{1,0:T(8,128)(2,1)S(1)}, bf16[384,256]{1,0:T(8,128)(2,1)S(1)}, u32[]{:S(2)}, u32[]{:S(2)}) collective-permute-start(bf16[384,256]{1,0:T(8,128)(2,1)S(1)} %get-tuple-element.25), channel_id=1, source_target_pairs={{0,16},{2,18},{4,20},{6,22},{8,24},{10,26},{12,28},{14,30},{16,0},... | collective-permute-start | bytes 589832 | tf_op jit(solution)/shard_map/ppermute | solution.py:383
  24.4 13.9 %collective-permute-done.1 = bf16[4,384,256]{2,1,0:T(8,128)(2,1)} collective-permute-done((bf16[4,384,256]{2,1,0:T(8,128)(2,1)}, bf16[4,384,256]{2,1,0:T(8,128)(2,1)}, u32[]{:S(2)}, u32[]{:S(2)}) %collective-permute-start.1) | collective-permute-done | bytes 786464 | tf_op jit(solution)/shard_map/ppermute | solution.py:383
  38.4 1.7 add_convert_fusion.1
  40.1 1.3 collective-permute-start.2
  41.6 2.3 %collective-permute-start.3 = (bf16[384,256]{1,0:T(8,128)(2,1)S(1)}, bf16[384,256]{1,0:T(8,128)(2,1)S(1)}, u32[]{:S(2)}, u32[]{:S(2)}) collective-permute-start(bf16[384,256]{1,0:T(8,128)(2,1)S(1)} %get-tuple-element.28), channel_id=1, source_target_pairs={{0,16},{2,18},{4,20},{6,22},{8,24},{10,26},{12,28},{14,30},{16,0},... | collective-permute-start | bytes 589832 | tf_op jit(solution)/shard_map/ppermute | solution.py:383
  44.0 1.3 collective-permute-start.9
  45.4 7.9 %collective-permute-done.4 = bf16[384,256]{1,0:T(8,128)(2,1)S(1)} collective-permute-done((bf16[384,256]{1,0:T(8,128)(2,1)S(1)}, bf16[384,256]{1,0:T(8,128)(2,1)S(1)}, u32[]{:S(2)}, u32[]{:S(2)}) %collective-permute-start.4) | collective-permute-done | bytes 196640 | tf_op jit(solution)/shard_map/ppermute | solution.py:383
  53.3 3.8 %collective-permute-done.3 = bf16[384,256]{1,0:T(8,128)(2,1)S(1)} collective-permute-done((bf16[384,256]{1,0:T(8,128)(2,1)S(1)}, bf16[384,256]{1,0:T(8,128)(2,1)S(1)}, u32[]{:S(2)}, u32[]{:S(2)}) %collective-permute-start.3) | collective-permute-done | bytes 196640 | tf_op jit(solution)/shard_map/ppermute | solution.py:383
  57.2 1.3 collective-permute-start.5
  58.6 2.4 %collective-permute-start.12 = (bf16[384,256]{1,0:T(8,128)(2,1)S(1)}, bf16[384,256]{1,0:T(8,128)(2,1)S(1)}, u32[]{:S(2)}, u32[]{:S(2)}) collective-permute-start(bf16[384,256]{1,0:T(8,128)(2,1)S(1)} %add_convert_fusion.3.refs_4_), channel_id=1, source_target_pairs={{0,2},{2,0},{4,6},{6,4},{8,10},{10,8},{12,14},{14,12},{16,18},{18,... | collective-permute-start | bytes 589832 | tf_op jit(solution)/shard_map/ppermute | solution.py:383
  61.1 0.7 collective-permute-done.5.refs_3_
  61.8 3.2 %collective-permute-start.11 = (bf16[384,256]{1,0:T(8,128)(2,1)S(1)}, bf16[384,256]{1,0:T(8,128)(2,1)S(1)}, u32[]{:S(2)}, u32[]{:S(2)}) collective-permute-start(bf16[384,256]{1,0:T(8,128)(2,1)S(1)} %collective-permute-done.5.refs_3_), channel_id=1, source_target_pairs={{0,2},{2,0},{4,6},{6,4},{8,10},{10,8},{12,14},{14,12},{16,18},{18,... | collective-permute-start | bytes 589832 | tf_op jit(solution)/shard_map/ppermute | solution.py:383
  65.1 1.0 collective-permute-done.11.refs_6_
  66.2 0.7 copy-done.17
  66.8 2.8 %assemble.1 = (bf16[2304,256]{1,0:T(8,128)(2,1)}, f32[8,128]{1,0:T(8,128)}) custom-call(s32[17]{0:T(128)} %stack.67.info.refs_0_, f32[1]{0:T(128)} %bitcast.17.refs_1_.refs_0_, bf16[384,256]{1,0:T(8,128)(2,1)} %copy-done, bf16[384,256]{1,0:T(8,128)(2,1)} %copy-done.14, bf16[384,256]{1,0:T(8,128)(2,1)} %copy-done.1, bf16[384,256]{1,0:T(8,128)(2,1)} %copy-done.16, ...), custom_call_target="tpu_custom_call" | custom-call | tf_op jit(solution)/shard_map/assemble/pallas_call | solution.py:357
  69.6 4.1 %collective-permute-start.13 = (f32[8,128]{1,0:T(8,128)}, f32[8,128]{1,0:T(8,128)S(1)}, u32[]{:S(2)}, u32[]{:S(2)}) collective-permute-start(f32[8,128]{1,0:T(8,128)} %get-tuple-element.15), channel_id=1, source_target_pairs={{0,8},{2,10},{4,12},{6,14},{8,0},{10,2},{12,4},{14,6},{16,24},{18,... | collective-permute-start | bytes 12296 | tf_op jit(solution)/shard_map/ppermute | solution.py:383
  73.7 1.2 collective-permute-done.13
  74.9 0.7 max.9
  76.0 2.9 %collective-permute-done.14 = f32[8,128]{1,0:T(8,128)S(1)} collective-permute-done((f32[8,128]{1,0:T(8,128)S(1)}, f32[8,128]{1,0:T(8,128)S(1)}, u32[]{:S(2)}, u32[]{:S(2)}) %collective-permute-start.14) | collective-permute-done | bytes 4128 | tf_op jit(solution)/shard_map/ppermute | solution.py:383
  78.9 1.2 collective-permute-start.15
  80.1 7.3 %powers.1 = (bf16[1024,1024]{1,0:T(8,128)(2,1)}, bf16[1024,1024]{1,0:T(8,128)(2,1)}) custom-call(f32[1]{0:T(128)} %bitcast.17.refs_1_.refs_0_, bf16[2304,256]{1,0:T(8,128)(2,1)} %get-tuple-element.16.refs_1_.refs_3_), custom_call_target="tpu_custom_call" | custom-call | flops 4294967296 | bytes 6291456 | tf_op jit(solution)/shard_map/powers/pallas_call | solution.py:173
  87.4 0.6 max.11.refs_2_
  88.0 12.0 %finish.1 = (bf16[2304,256]{1,0:T(8,128)(2,1)}, bf16[576,256]{1,0:T(8,128)(2,1)}) custom-call(s32[17]{0:T(128)} %stack.67.info.refs_0_, f32[1]{0:T(128)} %bitcast.17.refs_1_.refs_0_, f32[8,128]{1,0:T(8,128)} %max.11.refs_2_, bf16[2304,256]{1,0:T(8,128)(2,1)} %get-tuple-element.16.refs_1_.refs_3_, bf16[1024,1024]{1,0:T(8,128)(2,1)} %get-tuple-element.17.refs_4_, ...), custom_call_target="tpu_custom_call" | custom-call | tf_op jit(solution)/shard_map/finish/pallas_call | solution.py:224
  100.1 1.5 collective-permute-start.24
  101.6 1.4 collective-permute-start.16
  102.9 3.3 %collective-permute-done.24.refs_9_ = bf16[576,256]{1,0:T(8,128)(2,1)S(1)} collective-permute-done((bf16[576,256]{1,0:T(8,128)(2,1)}, bf16[576,256]{1,0:T(8,128)(2,1)S(1)}, u32[]{:S(2)}, u32[]{:S(2)}) %collective-permute-start.24) | collective-permute-done | bytes 294944 | tf_op jit(solution)/shard_map/ppermute | solution.py:383
  106.2 19.3 %collective-permute-start.26 = (bf16[576,256]{1,0:T(8,128)(2,1)S(1)}, bf16[576,256]{1,0:T(8,128)(2,1)S(1)}, u32[]{:S(2)}, u32[]{:S(2)}) collective-permute-start(bf16[576,256]{1,0:T(8,128)(2,1)S(1)} %collective-permute-done.24.refs_9_), channel_id=1, source_target_pairs={{0,2},{2,0},{4,6},{6,4},{8,10},{10,8},{12,14},{14,12},{16,18},{18,... | collective-permute-start | bytes 884744 | tf_op jit(solution)/shard_map/ppermute | solution.py:383
  125.5 1.2 collective-permute-start.25
  127.0 0.5 collective-permute-done.16.refs_1_
  127.5 1.2 collective-permute-start.17
  128.8 0.8 collective-permute-start.22
  129.6 4.5 %collective-permute-done.25.refs_10_ = bf16[576,256]{1,0:T(8,128)(2,1)S(1)} collective-permute-done((bf16[576,256]{1,0:T(8,128)(2,1)S(1)}, bf16[576,256]{1,0:T(8,128)(2,1)S(1)}, u32[]{:S(2)}, u32[]{:S(2)}) %collective-permute-start.25) | collective-permute-done | bytes 294944 | tf_op jit(solution)/shard_map/ppermute | solution.py:383
  134.1 1.3 collective-permute-start.27
  135.4 5.0 %collective-permute-done.21.refs_6_ = bf16[576,256]{1,0:T(8,128)(2,1)S(1)} collective-permute-done((bf16[576,256]{1,0:T(8,128)(2,1)S(1)}, bf16[576,256]{1,0:T(8,128)(2,1)S(1)}, u32[]{:S(2)}, u32[]{:S(2)}) %collective-permute-start.21) | collective-permute-done | bytes 294944 | tf_op jit(solution)/shard_map/ppermute | solution.py:383
  140.4 1.3 collective-permute-start.23
  141.7 5.0 %collective-permute-done.17.refs_2_ = bf16[576,256]{1,0:T(8,128)(2,1)S(1)} collective-permute-done((bf16[576,256]{1,0:T(8,128)(2,1)S(1)}, bf16[576,256]{1,0:T(8,128)(2,1)S(1)}, u32[]{:S(2)}, u32[]{:S(2)}) %collective-permute-start.17) | collective-permute-done | bytes 294944 | tf_op jit(solution)/shard_map/ppermute | solution.py:383
  146.7 0.9 collective-permute-start.19
  147.6 8.5 %apply.2.refs_14_ = f32[4096,1792]{1,0:T(8,128)} custom-call(s32[17]{0:T(128)} %stack.67.info.refs_0_, bf16[2304,256]{1,0:T(8,128)(2,1)} %get-tuple-element.20.refs_1_, bf16[2,4096,1792]{2,1,0:T(8,128)(2,1)} %refs_13_.1), custom_call_target="tpu_custom_call" | custom-call | flops 3758096384 | bytes 11010048 | tf_op jit(solution)/shard_map/apply/pallas_call | solution.py:300
  156.2 0.6 copy-done.9
  157.2 0.7 copy-done.13
  157.9 18.1 %apply.3 = f32[4096,1792]{1,0:T(8,128)} custom-call(s32[17]{0:T(128)} %stack.67.info.refs_0_, bf16[576,256]{1,0:T(8,128)(2,1)} %copy-done.4, bf16[576,256]{1,0:T(8,128)(2,1)} %copy-done.8, bf16[576,256]{1,0:T(8,128)(2,1)} %copy-done.10, bf16[576,256]{1,0:T(8,128)(2,1)} %copy-done.13, bf16[576,256]{1,0:T(8,128)(2,1)} %copy-done.3, ...), custom_call_target="tpu_custom_call", output_to_operand_aliasing={{}: (14, {})} | custom-call | flops 11274289152 | bytes 33030144 | tf_op jit(solution)/shard_map/apply/pallas_call | solution.py:300
  (61 shorter events, 2.0 us)
Async XLA Ops:
  11.6 5.0 %collective-permute-start = (bf16[4,1152,256]{2,1,0:T(8,128)(2,1)}, bf16[4,1152,256]{2,1,0:T(8,128)(2,1)S(1)}, u32[]{:S(2)}, u32[]{:S(2)}) collective-permute-start(bf16[4,1152,256]{2,1,0:T(8,128)(2,1)} %get-tuple-element.14), channel_id=1, source_target_pairs={{0,2},{2,0},{4,6},{6,4},{8,10},{10,8},{12,14},{14,12},{16,18},{18,... | collective-permute-start | bytes 7077896 | tf_op jit(solution)/shard_map/ppermute | solution.py:383
  19.3 19.0 %collective-permute-start.1 = (bf16[4,384,256]{2,1,0:T(8,128)(2,1)}, bf16[4,384,256]{2,1,0:T(8,128)(2,1)}, u32[]{:S(2)}, u32[]{:S(2)}) collective-permute-start(bf16[4,384,256]{2,1,0:T(8,128)(2,1)} %get-tuple-element.22), channel_id=1, source_target_pairs={{0,4},{2,6},{4,0},{6,2},{8,12},{10,14},{12,8},{14,10},{16,20},{18,... | collective-permute-start | bytes 2359304 | tf_op jit(solution)/shard_map/ppermute | solution.py:383
  20.6 21.0 %collective-permute-start.6 = (bf16[384,256]{1,0:T(8,128)(2,1)S(1)}, bf16[384,256]{1,0:T(8,128)(2,1)S(1)}, u32[]{:S(2)}, u32[]{:S(2)}) collective-permute-start(bf16[384,256]{1,0:T(8,128)(2,1)S(1)} %get-tuple-element.23), channel_id=1, source_target_pairs={{0,8},{2,10},{4,12},{6,14},{8,16},{10,18},{12,20},{14,22},{16,24},... | collective-permute-start | bytes 589832 | tf_op jit(solution)/shard_map/ppermute | solution.py:383
  22.0 22.0 %collective-permute-start.8 = (bf16[384,256]{1,0:T(8,128)(2,1)S(1)}, bf16[384,256]{1,0:T(8,128)(2,1)S(1)}, u32[]{:S(2)}, u32[]{:S(2)}) collective-permute-start(bf16[384,256]{1,0:T(8,128)(2,1)S(1)} %get-tuple-element.24), channel_id=1, source_target_pairs={{0,24},{2,26},{4,28},{6,30},{8,0},{10,2},{12,4},{14,6},{16,8},{18,... | collective-permute-start | bytes 589832 | tf_op jit(solution)/shard_map/ppermute | solution.py:383
  22.1 21.8 %collective-permute-start.7 = (bf16[384,256]{1,0:T(8,128)(2,1)S(1)}, bf16[384,256]{1,0:T(8,128)(2,1)S(1)}, u32[]{:S(2)}, u32[]{:S(2)}) collective-permute-start(bf16[384,256]{1,0:T(8,128)(2,1)S(1)} %get-tuple-element.25), channel_id=1, source_target_pairs={{0,16},{2,18},{4,20},{6,22},{8,24},{10,26},{12,28},{14,30},{16,0},... | collective-permute-start | bytes 589832 | tf_op jit(solution)/shard_map/ppermute | solution.py:383
  40.1 5.3 %collective-permute-start.2 = (bf16[384,256]{1,0:T(8,128)(2,1)S(1)}, bf16[384,256]{1,0:T(8,128)(2,1)S(1)}, u32[]{:S(2)}, u32[]{:S(2)}) collective-permute-start(bf16[384,256]{1,0:T(8,128)(2,1)S(1)} %get-tuple-element.26), channel_id=1, source_target_pairs={{0,8},{2,10},{4,12},{6,14},{8,16},{10,18},{12,20},{14,22},{16,24},... | collective-permute-start | bytes 589832 | tf_op jit(solution)/shard_map/ppermute | solution.py:383
  41.4 11.9 %collective-permute-start.4 = (bf16[384,256]{1,0:T(8,128)(2,1)S(1)}, bf16[384,256]{1,0:T(8,128)(2,1)S(1)}, u32[]{:S(2)}, u32[]{:S(2)}) collective-permute-start(bf16[384,256]{1,0:T(8,128)(2,1)S(1)} %get-tuple-element.27), channel_id=1, source_target_pairs={{0,24},{2,26},{4,28},{6,30},{8,0},{10,2},{12,4},{14,6},{16,8},{18,... | collective-permute-start | bytes 589832 | tf_op jit(solution)/shard_map/ppermute | solution.py:383
  41.6 15.5 %collective-permute-start.3 = (bf16[384,256]{1,0:T(8,128)(2,1)S(1)}, bf16[384,256]{1,0:T(8,128)(2,1)S(1)}, u32[]{:S(2)}, u32[]{:S(2)}) collective-permute-start(bf16[384,256]{1,0:T(8,128)(2,1)S(1)} %get-tuple-element.28), channel_id=1, source_target_pairs={{0,16},{2,18},{4,20},{6,22},{8,24},{10,26},{12,28},{14,30},{16,0},... | collective-permute-start | bytes 589832 | tf_op jit(solution)/shard_map/ppermute | solution.py:383
  44.0 14.5 %collective-permute-start.9 = (bf16[384,256]{1,0:T(8,128)(2,1)S(1)}, bf16[384,256]{1,0:T(8,128)(2,1)S(1)}, u32[]{:S(2)}, u32[]{:S(2)}) collective-permute-start(bf16[384,256]{1,0:T(8,128)(2,1)S(1)} %fusion.2), channel_id=1, source_target_pairs={{0,4},{2,6},{4,0},{6,2},{8,12},{10,14},{12,8},{14,10},{16,20},{18,... | collective-permute-start | bytes 589832 | tf_op jit(solution)/shard_map/ppermute | solution.py:383
  57.2 8.9 %copy-start = (bf16[384,256]{1,0:T(8,128)(2,1)}, bf16[384,256]{1,0:T(8,128)(2,1)S(1)}, u32[]{:S(2)}) copy-start(bf16[384,256]{1,0:T(8,128)(2,1)S(1)} %fusion.5.refs_2_) | copy-start | bytes 589828
  57.2 4.6 %collective-permute-start.5 = (bf16[384,256]{1,0:T(8,128)(2,1)S(1)}, bf16[384,256]{1,0:T(8,128)(2,1)S(1)}, u32[]{:S(2)}, u32[]{:S(2)}) collective-permute-start(bf16[384,256]{1,0:T(8,128)(2,1)S(1)} %fusion.5.refs_2_), channel_id=1, source_target_pairs={{0,4},{2,6},{4,0},{6,2},{8,12},{10,14},{12,8},{14,10},{16,20},{18,... | collective-permute-start | bytes 589832 | tf_op jit(solution)/shard_map/ppermute | solution.py:383
  58.6 7.5 %copy-start.1 = (bf16[384,256]{1,0:T(8,128)(2,1)}, bf16[384,256]{1,0:T(8,128)(2,1)S(1)}, u32[]{:S(2)}) copy-start(bf16[384,256]{1,0:T(8,128)(2,1)S(1)} %add_convert_fusion.3.refs_4_) | copy-start | bytes 589828
  58.6 6.4 %collective-permute-start.12 = (bf16[384,256]{1,0:T(8,128)(2,1)S(1)}, bf16[384,256]{1,0:T(8,128)(2,1)S(1)}, u32[]{:S(2)}, u32[]{:S(2)}) collective-permute-start(bf16[384,256]{1,0:T(8,128)(2,1)S(1)} %add_convert_fusion.3.refs_4_), channel_id=1, source_target_pairs={{0,2},{2,0},{4,6},{6,4},{8,10},{10,8},{12,14},{14,12},{16,18},{18,... | collective-permute-start | bytes 589832 | tf_op jit(solution)/shard_map/ppermute | solution.py:383
  61.0 4.0 %collective-permute-start.10 = (bf16[384,256]{1,0:T(8,128)(2,1)S(1)}, bf16[384,256]{1,0:T(8,128)(2,1)S(1)}, u32[]{:S(2)}, u32[]{:S(2)}) collective-permute-start(bf16[384,256]{1,0:T(8,128)(2,1)S(1)} %fusion.5.refs_2_), channel_id=1, source_target_pairs={{0,2},{2,0},{4,6},{6,4},{8,10},{10,8},{12,14},{14,12},{16,18},{18,... | collective-permute-start | bytes 589832 | tf_op jit(solution)/shard_map/ppermute | solution.py:383
  61.8 4.3 %copy-start.14 = (bf16[384,256]{1,0:T(8,128)(2,1)}, bf16[384,256]{1,0:T(8,128)(2,1)S(1)}, u32[]{:S(2)}) copy-start(bf16[384,256]{1,0:T(8,128)(2,1)S(1)} %collective-permute-done.5.refs_3_) | copy-start | bytes 589828
  61.8 4.3 %collective-permute-start.11 = (bf16[384,256]{1,0:T(8,128)(2,1)S(1)}, bf16[384,256]{1,0:T(8,128)(2,1)S(1)}, u32[]{:S(2)}, u32[]{:S(2)}) collective-permute-start(bf16[384,256]{1,0:T(8,128)(2,1)S(1)} %collective-permute-done.5.refs_3_), channel_id=1, source_target_pairs={{0,2},{2,0},{4,6},{6,4},{8,10},{10,8},{12,14},{14,12},{16,18},{18,... | collective-permute-start | bytes 589832 | tf_op jit(solution)/shard_map/ppermute | solution.py:383
  65.1 1.1 copy-start.15
  65.1 1.1 copy-start.16
  66.1 0.7 copy-start.17
  69.6 5.3 %collective-permute-start.13 = (f32[8,128]{1,0:T(8,128)}, f32[8,128]{1,0:T(8,128)S(1)}, u32[]{:S(2)}, u32[]{:S(2)}) collective-permute-start(f32[8,128]{1,0:T(8,128)} %get-tuple-element.15), channel_id=1, source_target_pairs={{0,8},{2,10},{4,12},{6,14},{8,0},{10,2},{12,4},{14,6},{16,24},{18,... | collective-permute-start | bytes 12296 | tf_op jit(solution)/shard_map/ppermute | solution.py:383
  75.5 3.4 %collective-permute-start.14 = (f32[8,128]{1,0:T(8,128)S(1)}, f32[8,128]{1,0:T(8,128)S(1)}, u32[]{:S(2)}, u32[]{:S(2)}) collective-permute-start(f32[8,128]{1,0:T(8,128)S(1)} %max.9), channel_id=1, source_target_pairs={{0,16},{2,18},{4,20},{6,22},{8,24},{10,26},{12,28},{14,30},{16,0},... | collective-permute-start | bytes 12296 | tf_op jit(solution)/shard_map/ppermute | solution.py:383
  78.9 8.6 %collective-permute-start.15 = (f32[8,128]{1,0:T(8,128)S(1)}, f32[8,128]{1,0:T(8,128)S(1)}, u32[]{:S(2)}, u32[]{:S(2)}) collective-permute-start(f32[8,128]{1,0:T(8,128)S(1)} %max.10), channel_id=1, source_target_pairs={{0,1},{1,0},{2,3},{3,2},{4,5},{5,4},{6,7},{7,6},{8,9},{9,8},{10,11... | collective-permute-start | bytes 12296 | tf_op jit(solution)/shard_map/ppermute | solution.py:442
  100.1 6.2 %collective-permute-start.24 = (bf16[576,256]{1,0:T(8,128)(2,1)}, bf16[576,256]{1,0:T(8,128)(2,1)S(1)}, u32[]{:S(2)}, u32[]{:S(2)}) collective-permute-start(bf16[576,256]{1,0:T(8,128)(2,1)} %get-tuple-element.19), channel_id=1, source_target_pairs={{0,24},{2,26},{4,28},{6,30},{8,0},{10,2},{12,4},{14,6},{16,8},{18,... | collective-permute-start | bytes 884744 | tf_op jit(solution)/shard_map/ppermute | solution.py:383
  101.6 25.2 %collective-permute-start.20 = (bf16[576,256]{1,0:T(8,128)(2,1)}, bf16[576,256]{1,0:T(8,128)(2,1)S(1)}, u32[]{:S(2)}, u32[]{:S(2)}) collective-permute-start(bf16[576,256]{1,0:T(8,128)(2,1)} %get-tuple-element.19), channel_id=1, source_target_pairs={{0,16},{2,18},{4,20},{6,22},{8,24},{10,26},{12,28},{14,30},{16,0},... | collective-permute-start | bytes 884744 | tf_op jit(solution)/shard_map/ppermute | solution.py:383
  101.6 25.9 %collective-permute-start.16 = (bf16[576,256]{1,0:T(8,128)(2,1)}, bf16[576,256]{1,0:T(8,128)(2,1)S(1)}, u32[]{:S(2)}, u32[]{:S(2)}) collective-permute-start(bf16[576,256]{1,0:T(8,128)(2,1)} %get-tuple-element.19), channel_id=1, source_target_pairs={{0,8},{2,10},{4,12},{6,14},{8,16},{10,18},{12,20},{14,22},{16,24},... | collective-permute-start | bytes 884744 | tf_op jit(solution)/shard_map/ppermute | solution.py:383
  106.2 49.8 %copy-start.2 = (bf16[576,256]{1,0:T(8,128)(2,1)}, bf16[576,256]{1,0:T(8,128)(2,1)S(1)}, u32[]{:S(2)}) copy-start(bf16[576,256]{1,0:T(8,128)(2,1)S(1)} %collective-permute-done.24.refs_9_) | copy-start | bytes 884740
  106.2 23.3 %collective-permute-start.26 = (bf16[576,256]{1,0:T(8,128)(2,1)S(1)}, bf16[576,256]{1,0:T(8,128)(2,1)S(1)}, u32[]{:S(2)}, u32[]{:S(2)}) collective-permute-start(bf16[576,256]{1,0:T(8,128)(2,1)S(1)} %collective-permute-done.24.refs_9_), channel_id=1, source_target_pairs={{0,2},{2,0},{4,6},{6,4},{8,10},{10,8},{12,14},{14,12},{16,18},{18,... | collective-permute-start | bytes 884744 | tf_op jit(solution)/shard_map/ppermute | solution.py:383
  125.5 8.6 %collective-permute-start.25 = (bf16[576,256]{1,0:T(8,128)(2,1)S(1)}, bf16[576,256]{1,0:T(8,128)(2,1)S(1)}, u32[]{:S(2)}, u32[]{:S(2)}) collective-permute-start(bf16[576,256]{1,0:T(8,128)(2,1)S(1)} %collective-permute-done.24.refs_9_), channel_id=1, source_target_pairs={{0,4},{2,6},{4,0},{6,2},{8,12},{10,14},{12,8},{14,10},{16,20},{18,... | collective-permute-start | bytes 884744 | tf_op jit(solution)/shard_map/ppermute | solution.py:383
  126.7 29.3 %copy-start.3 = (bf16[576,256]{1,0:T(8,128)(2,1)}, bf16[576,256]{1,0:T(8,128)(2,1)S(1)}, u32[]{:S(2)}) copy-start(bf16[576,256]{1,0:T(8,128)(2,1)S(1)} %collective-permute-done.20.refs_5_) | copy-start | bytes 884740
  126.8 13.6 %collective-permute-start.21 = (bf16[576,256]{1,0:T(8,128)(2,1)S(1)}, bf16[576,256]{1,0:T(8,128)(2,1)S(1)}, u32[]{:S(2)}, u32[]{:S(2)}) collective-permute-start(bf16[576,256]{1,0:T(8,128)(2,1)S(1)} %collective-permute-done.20.refs_5_), channel_id=1, source_target_pairs={{0,4},{2,6},{4,0},{6,2},{8,12},{10,14},{12,8},{14,10},{16,20},{18,... | collective-permute-start | bytes 884744 | tf_op jit(solution)/shard_map/ppermute | solution.py:383
  127.5 28.6 %copy-start.4 = (bf16[576,256]{1,0:T(8,128)(2,1)}, bf16[576,256]{1,0:T(8,128)(2,1)S(1)}, u32[]{:S(2)}) copy-start(bf16[576,256]{1,0:T(8,128)(2,1)S(1)} %collective-permute-done.16.refs_1_) | copy-start | bytes 884740
  127.5 19.2 %collective-permute-start.17 = (bf16[576,256]{1,0:T(8,128)(2,1)S(1)}, bf16[576,256]{1,0:T(8,128)(2,1)S(1)}, u32[]{:S(2)}, u32[]{:S(2)}) collective-permute-start(bf16[576,256]{1,0:T(8,128)(2,1)S(1)} %collective-permute-done.16.refs_1_), channel_id=1, source_target_pairs={{0,4},{2,6},{4,0},{6,2},{8,12},{10,14},{12,8},{14,10},{16,20},{18,... | collective-permute-start | bytes 884744 | tf_op jit(solution)/shard_map/ppermute | solution.py:383
  128.8 27.4 %collective-permute-start.22 = (bf16[576,256]{1,0:T(8,128)(2,1)S(1)}, bf16[576,256]{1,0:T(8,128)(2,1)S(1)}, u32[]{:S(2)}, u32[]{:S(2)}) collective-permute-start(bf16[576,256]{1,0:T(8,128)(2,1)S(1)} %collective-permute-done.20.refs_5_), channel_id=1, source_target_pairs={{0,2},{2,0},{4,6},{6,4},{8,10},{10,8},{12,14},{14,12},{16,18},{18,... | collective-permute-start | bytes 884744 | tf_op jit(solution)/shard_map/ppermute | solution.py:383
  129.5 26.6 %copy-start.5 = (bf16[576,256]{1,0:T(8,128)(2,1)}, bf16[576,256]{1,0:T(8,128)(2,1)S(1)}, u32[]{:S(2)}) copy-start(bf16[576,256]{1,0:T(8,128)(2,1)S(1)} %collective-permute-done.26.refs_11_) | copy-start | bytes 884740
  129.5 26.6 %collective-permute-start.18 = (bf16[576,256]{1,0:T(8,128)(2,1)S(1)}, bf16[576,256]{1,0:T(8,128)(2,1)S(1)}, u32[]{:S(2)}, u32[]{:S(2)}) collective-permute-start(bf16[576,256]{1,0:T(8,128)(2,1)S(1)} %collective-permute-done.16.refs_1_), channel_id=1, source_target_pairs={{0,2},{2,0},{4,6},{6,4},{8,10},{10,8},{12,14},{14,12},{16,18},{18,... | collective-permute-start | bytes 884744 | tf_op jit(solution)/shard_map/ppermute | solution.py:383
  134.1 22.0 %copy-start.6 = (bf16[576,256]{1,0:T(8,128)(2,1)}, bf16[576,256]{1,0:T(8,128)(2,1)S(1)}, u32[]{:S(2)}) copy-start(bf16[576,256]{1,0:T(8,128)(2,1)S(1)} %collective-permute-done.25.refs_10_) | copy-start | bytes 884740
  134.1 22.1 %collective-permute-start.27 = (bf16[576,256]{1,0:T(8,128)(2,1)S(1)}, bf16[576,256]{1,0:T(8,128)(2,1)S(1)}, u32[]{:S(2)}, u32[]{:S(2)}) collective-permute-start(bf16[576,256]{1,0:T(8,128)(2,1)S(1)} %collective-permute-done.25.refs_10_), channel_id=1, source_target_pairs={{0,2},{2,0},{4,6},{6,4},{8,10},{10,8},{12,14},{14,12},{16,18},{18,... | collective-permute-start | bytes 884744 | tf_op jit(solution)/shard_map/ppermute | solution.py:383
  140.4 15.7 %copy-start.7 = (bf16[576,256]{1,0:T(8,128)(2,1)}, bf16[576,256]{1,0:T(8,128)(2,1)S(1)}, u32[]{:S(2)}) copy-start(bf16[576,256]{1,0:T(8,128)(2,1)S(1)} %collective-permute-done.21.refs_6_) | copy-start | bytes 884740
  140.4 15.8 %collective-permute-start.23 = (bf16[576,256]{1,0:T(8,128)(2,1)S(1)}, bf16[576,256]{1,0:T(8,128)(2,1)S(1)}, u32[]{:S(2)}, u32[]{:S(2)}) collective-permute-start(bf16[576,256]{1,0:T(8,128)(2,1)S(1)} %collective-permute-done.21.refs_6_), channel_id=1, source_target_pairs={{0,2},{2,0},{4,6},{6,4},{8,10},{10,8},{12,14},{14,12},{16,18},{18,... | collective-permute-start | bytes 884744 | tf_op jit(solution)/shard_map/ppermute | solution.py:383
  146.7 9.4 %copy-start.8 = (bf16[576,256]{1,0:T(8,128)(2,1)}, bf16[576,256]{1,0:T(8,128)(2,1)S(1)}, u32[]{:S(2)}) copy-start(bf16[576,256]{1,0:T(8,128)(2,1)S(1)} %collective-permute-done.17.refs_2_) | copy-start | bytes 884740
  146.7 9.5 %collective-permute-start.19 = (bf16[576,256]{1,0:T(8,128)(2,1)S(1)}, bf16[576,256]{1,0:T(8,128)(2,1)S(1)}, u32[]{:S(2)}, u32[]{:S(2)}) collective-permute-start(bf16[576,256]{1,0:T(8,128)(2,1)S(1)} %collective-permute-done.17.refs_2_), channel_id=1, source_target_pairs={{0,2},{2,0},{4,6},{6,4},{8,10},{10,8},{12,14},{14,12},{16,18},{18,... | collective-permute-start | bytes 884744 | tf_op jit(solution)/shard_map/ppermute | solution.py:383
  156.1 0.7 copy-start.9
  156.2 0.8 copy-start.10
  156.2 0.9 copy-start.11
  156.2 1.0 copy-start.12
  157.2 0.7 copy-start.13

commit v2 on v1

--- a/solution.py
+++ b/solution.py
@@ -11,20 +11,27 @@
 TILE = 256
 HALF = TILE // 2
 NT = BLOCK // TILE
+QUARTS = ((0, 0), (0, HALF), (HALF, HALF))
+SLOT = {}
+SLOT.update({(0, j): j - 1 for j in range(1, NT)})
+SLOT[0, 0] = NT - 1
 OFF = [(i, j) for i in range(NT) for j in range(i + 1, NT)]
-SLOTS = len(OFF) + NT - 1
-ROWS = SLOTS * TILE
-QUARTS = ((0, 0), (0, HALF), (HALF, HALF))
-DIAG0 = len(OFF)
+for _n, _t in enumerate([t for t in OFF if t[0] > 0] + [(d, d) for d in range(1, NT - 1)]):
+    SLOT[_t] = NT + _n
+DIAGS = [SLOT[d, d] for d in range(NT - 1)]
+ROWS = len(SLOT) * TILE
+EARLY = NT * TILE
+UNIT = 64
 LIMIT = 60 * 1024 * 1024
 
 
 def pack(dst, tile_of):
-    for s, (i, j) in enumerate(OFF):
+    for i, j in OFF:
+        s = SLOT[i, j]
         dst[s * TILE:(s + 1) * TILE, :] = tile_of(i, j).astype(dst.dtype)
     last = tile_of(NT - 1, NT - 1).astype(dst.dtype)
     for d in range(NT - 1):
-        r = (DIAG0 + d) * TILE
+        r = DIAGS[d] * TILE
         t = tile_of(d, d).astype(dst.dtype)
         dst[r:r + HALF, :] = t[:HALF, :]
         dst[r + HALF:r + TILE, HALF:] = t[HALF:, HALF:]
@@ -33,12 +40,13 @@
 
 
 def unpack(src, put, dtype):
-    for s, (i, j) in enumerate(OFF):
+    for i, j in OFF:
+        s = SLOT[i, j]
         t = src[s * TILE:(s + 1) * TILE, :].astype(dtype)
         put(i * TILE, j * TILE, t)
         put(j * TILE, i * TILE, t.T)
     for d in range(NT - 1):
-        r = (DIAG0 + d) * TILE
+        r = DIAGS[d] * TILE
         o = d * TILE
         upper = src[r:r + HALF, HALF:].astype(dtype)
         put(o, o, src[r:r + HALF, :HALF].astype(dtype))
@@ -57,42 +65,49 @@
     return lax.dot_general(a, b, (dims, ((), ())), preferred_element_type=jnp.float32)
 
 
-def gram_body(info, acts, keep, send, scratch):
-    for i in range(NT):
+def gram_body(info, acts, keep, send, scratch, *, early, late):
+    base = 0 if early else EARLY
+    last = (NT - 1) * TILE
+
+    def put(row, col, v):
+        scratch[row:row + v.shape[0], col:col + v.shape[1]] = v.astype(scratch.dtype)
+
+    panels = ([0] if early else []) + (list(range(1, NT - 1)) if late else [])
+    for i in panels:
         panel = dot(acts[:, i * TILE:(i + 1) * TILE], acts[:, i * TILE:], ((0,), (0,)))
-        for s, (a, b) in enumerate(OFF):
-            if a == i:
-                o = (b - i) * TILE
-                scratch[s * TILE:(s + 1) * TILE, :] = panel[:, o:o + TILE].astype(scratch.dtype)
-        t = panel[:, :TILE].astype(scratch.dtype)
-        if i < NT - 1:
-            r = (DIAG0 + i) * TILE
-            scratch[r:r + HALF, :] = t[:HALF, :]
-            scratch[r + HALF:r + TILE, HALF:] = t[HALF:, HALF:]
-        else:
-            for d, (y, x) in enumerate(QUARTS):
-                r = (DIAG0 + d) * TILE
-                scratch[r + HALF:r + TILE, :HALF] = t[y:y + HALF, x:x + HALF]
+        for j in range(i + 1, NT):
+            o = (j - i) * TILE
+            put(SLOT[i, j] * TILE - base, 0, panel[:, o:o + TILE])
+        r = DIAGS[i] * TILE - base
+        put(r, 0, panel[:HALF, :TILE])
+        put(r + HALF, HALF, panel[HALF:, HALF:TILE])
+    if early:
+        corner = acts[:, last:last + HALF]
+        put(DIAGS[0] * TILE - base + HALF, 0, dot(corner, corner, ((0,), (0,))))
+    if late:
+        edge = dot(acts[:, last:], acts[:, last + HALF:], ((0,), (0,)))
+        put(DIAGS[1] * TILE - base + HALF, 0, edge[:HALF, :])
+        put(DIAGS[2] * TILE - base + HALF, 0, edge[HALF:, :])
     if send is None:
         keep[...] = scratch[...]
     else:
-        rows = ROWS // 2
+        rows = keep.shape[0]
         core = info[1]
         keep[...] = scratch[pl.ds(pl.multiple_of(core * rows, HALF), rows), :]
         send[...] = scratch[pl.ds(pl.multiple_of((1 - core) * rows, HALF), rows), :]
 
 
-def gram(info, activations, nblock, split):
+def gram(info, activations, nblock, split, early=True, late=True):
     tok = activations.shape[1]
-    rows = ROWS // 2 if split else ROWS
+    size = (EARLY if early else 0) + (ROWS - EARLY if late else 0)
+    rows = size // 2 if split else size
     spec = pl.BlockSpec((None, rows, TILE), lambda b, info: (b, 0, 0))
     shape = jax.ShapeDtypeStruct((nblock, rows, TILE), jnp.bfloat16)
 
     def body(info, acts, *rest):
-        if split:
-            gram_body(info, acts, *rest)
-        else:
-            gram_body(info, acts, rest[0], None, rest[1])
+        if not split:
+            rest = (rest[0], None, rest[1])
+        gram_body(info, acts, *rest, early=early, late=late)
 
     return pl.pallas_call(
         body,
@@ -101,10 +116,13 @@
             grid=(nblock,),
             in_specs=[pl.BlockSpec((None, tok, BLOCK), lambda b, info: (info[0], 0, b))],
             out_specs=[spec, spec] if split else [spec],
-            scratch_shapes=[pltpu.VMEM((ROWS, TILE), jnp.bfloat16)],
+            scratch_shapes=[pltpu.VMEM((size, TILE), jnp.bfloat16)],
         ),
         out_shape=[shape, shape] if split else [shape],
         compiler_params=pltpu.CompilerParams(vmem_limit_bytes=LIMIT),
+        cost_estimate=pl.CostEstimate(
+            flops=nblock * tok * BLOCK * BLOCK // 2, transcendentals=0, bytes_accessed=nblock * tok * BLOCK * 2
+        ),
         name="gram",
     )(info, activations)
 
@@ -113,11 +131,13 @@
     f = packed.astype(jnp.float32)
     r = lax.broadcasted_iota(jnp.int32, (ROWS, TILE), 0)
     c = lax.broadcasted_iota(jnp.int32, (ROWS, TILE), 1)
-    slot = r // TILE - DIAG0
+    slot = r // TILE
     rr = r % TILE
+    diag = (slot == DIAGS[0]) | (slot == DIAGS[1]) | (slot == DIAGS[2])
     low = (rr >= HALF) & (c < HALF)
-    on = ((low & (rr - HALF == c) & (slot != 1)) | (rr == c)) & (slot >= 0)
-    twice = (slot < 0) | (low & (slot == 1)) | ((rr < HALF) & (c >= HALF))
+    mixed = slot == DIAGS[1]
+    on = ((low & (rr - HALF == c) & ~mixed) | (rr == c)) & diag
+    twice = ~diag | (low & mixed) | ((rr < HALF) & (c >= HALF))
     f = f / tokens + jnp.where(on, damping, 0.0)
     return jnp.sum(f * f * jnp.where(twice, 2.0, 1.0))
 
@@ -346,10 +366,9 @@
 def assemble_body(info, damp, *refs, count, tokens, first):
     pieces = refs[:count]
     out, total = refs[count:]
-    n = ROWS // count
     for p, piece in enumerate(pieces):
-        start = pl.multiple_of(info[first + p] * n, 64)
-        out[pl.ds(start, n), :] = piece[...]
+        start = pl.multiple_of(info[first + p] * UNIT, UNIT)
+        out[pl.ds(start, piece.shape[0]), :] = piece[...]
     total[...] = jnp.full(total.shape, squares(out[...], damp[0], tokens), jnp.float32)
 
 
@@ -404,20 +423,23 @@
             total = total + p
         return total.astype(bf)
 
-    places = [3 * c + y, 3 * c + 1 - y, 3 * c + 2]
-    places += [3 * (1 - c) + y, 3 * (1 - c) + 1 - y, 3 * (1 - c) + 2]
+    third = ROWS // 6
+
+    def places_of(core):
+        start = 3 * core * third
+        return [(start + n * third) // UNIT for n in (y, 1 - y, 2)]
+
+    places = places_of(c) + places_of(1 - c)
     spread = [2 * c + y, 2 * c + 1 - y, 2 * (1 - c) + y, 2 * (1 - c) + 1 - y]
     blocks = [(z - k) % nblock for k in range(nblock)]
     info = jnp.stack([layer, c, *places, *spread, 0, *blocks]).astype(jnp.int32)
     keep, send = gram(info, activations, nblock, True)
     got = swap_c(send)
-    third = ROWS // 6
 
     def rows_of(v, start):
         return lax.dynamic_slice_in_dim(v, start, third, 1)
 
-    early = 2 * third
-    zpart = plus(keep[:, early:], got[:, early:])
+    zpart = plus(keep[:, 2 * third:], got[:, 2 * third:])
     other = (1 - y) * third
     mine = y * third
     ysend = plus(rows_of(keep, other), rows_of(got, other))
@@ -432,11 +454,11 @@
     damping = damping.reshape(1)
     packed, top = assemble(info, 2, damping, own + theirs, tokens)
 
-    d = 1
-    while d < nblock:
-        moved = move(top, lambda i: i ^ (4 * d))
-        top = jnp.maximum(top, moved)
-        d *= 2
+    tops = [top]
+    for k in range(1, nblock):
+        tops.append(shift(top, k))
+    for other in tops[1:]:
+        top = jnp.maximum(top, other)
     d = 1
     while d < halves:
         top = jnp.maximum(top, lax.ppermute(top, "tensor", [(i, i ^ d) for i in range(halves)]))
@@ -446,13 +468,15 @@
 
     arrived = []
     for k in range(1, nblock):
-        arrived.append(shift(piece, k))
+        arrived.append(shift(arrived[0], 1) if k == 2 and nblock == 4 else shift(piece, k))
     result = apply_blocks(info, [13], 12, [inverse], grad_weight, None)
     pieces = []
-    for a in arrived:
+    for k, a in zip(range(1, nblock), arrived):
         ya = swap_y(a)
-        pieces += [a, ya, swap_c(a), swap_c(ya)]
-    return apply_blocks(info, [13 + k for k in range(1, nblock)], 8, pieces, grad_weight, result)
+        pieces.append([a, ya, swap_c(a), swap_c(ya)])
+    result = apply_blocks(info, [12 + nblock], 8, pieces[-1], grad_weight, result)
+    rest = [p for four in pieces[:-1] for p in four]
+    return apply_blocks(info, [13 + k for k in range(1, nblock - 1)], 8, rest, grad_weight, result)
 
 
 def power_of_two(n):
@@ -464,7 +488,7 @@
 
     def local(step, activations, grad_weight):
         nblock = activations.shape[2] // BLOCK
-        quad = groups == 4 * nblock and nblock > 1 and power_of_two(groups) and power_of_two(halves)
+        quad = groups == 4 * nblock and nblock > 2 and power_of_two(groups) and power_of_two(halves)
         return (local_quad if quad else local_any)(step, activations, grad_weight)
 
     in_specs = (P(), P(None, "dp", "tensor"), P(None, "tensor", "dp"))

time: 177 us -> 162 us (0.915)
  the two profiles are of different devices: /device:TPU:9 before, /device:TPU:0 now
where the time goes in v2:
time: 162 us; the launch traced here: 161 us
  Pallas kernels  62.3 us (38%)
  waiting for transfers between devices  50.1 us (31%)
  starting transfers between devices  38.1 us (24%)
  other arithmetic  5.86 us (4%)
  local copies, waits for them, and re-layouts  3.72 us (2%)
    ppermute x28, waiting for transfers between devices, move(): return lax.ppermute(v, 'dp', [(i, f(i)) for i in range(groups)])  50.1 us
    ppermute x28, starting transfers between devices, move(): return lax.ppermute(v, 'dp', [(i, f(i)) for i in range(groups)])  36.6 us
    pallas_call x3, Pallas kernels, apply_blocks(): pl.pallas_call(lambda *refs: apply_body(*refs, count=count, blocks=blocks...  29.8 us
    pallas_call x1, Pallas kernels, finish(): pl.pallas_call(lambda *refs: finish_body(*refs, tokens=tokens), in_specs=...  12 us
    pallas_call x1, Pallas kernels, gram(): pl.pallas_call(body, grid_spec=pltpu.PrefetchScalarGridSpec(num_scalar_pr...  10.4 us
    pallas_call x1, Pallas kernels, powers(): pl.pallas_call(lambda *refs: powers_body(*refs, tokens=tokens), in_specs=...  7.32 us
  transfers between devices with their start and end apart: 29, of which 10 were waited for; matrix products, arithmetic and copies ran while one was open for 1% of the time, Pallas kernels for 15%

profile of v2, /device:TPU:0, one launch (start us, length us, event | category | flops | bytes accessed | tf_op | source)
XLA Modules:
  0.0 161.4 jit_solution(14771080716357594275)
XLA Ops:
  0.8 0.6 stack.67.info.refs_0_
  1.4 10.4 %gram.1 = (bf16[4,1152,256]{2,1,0:T(8,128)(2,1)}, bf16[4,1152,256]{2,1,0:T(8,128)(2,1)}) custom-call(s32[17]{0:T(128)} %stack.67.info.refs_0_, bf16[2,1024,4096]{2,1,0:T(8,128)(2,1)} %acts.1), custom_call_target="tpu_custom_call" | custom-call | flops 2147483648 | bytes 8388608 | tf_op jit(solution)/shard_map/gram/pallas_call | solution.py:112
  11.9 0.5 collective-permute-start
  12.4 4.4 %collective-permute-done = bf16[4,1152,256]{2,1,0:T(8,128)(2,1)S(1)} collective-permute-done((bf16[4,1152,256]{2,1,0:T(8,128)(2,1)}, bf16[4,1152,256]{2,1,0:T(8,128)(2,1)S(1)}, u32[]{:S(2)}, u32[]{:S(2)}) %collective-permute-start) | collective-permute-done | bytes 2359328 | tf_op jit(solution)/shard_map/ppermute | solution.py:402
  16.7 2.7 %add_convert_fusion = (bf16[4,384,256]{2,1,0:T(8,128)(2,1)S(1)}, bf16[4,384,256]{2,1,0:T(8,128)(2,1)}) fusion(bf16[4,1152,256]{2,1,0:T(8,128)(2,1)S(1)} %collective-permute-done, bf16[4,1152,256]{2,1,0:T(8,128)(2,1)} %get-tuple-element.13, s32[]{:T(128)S(6)} %select_n.115), kind=kLoop, calls=%fused_computation | loop fusion | flops 3145728 | bytes 4718596 | tf_op jit(solution)/shard_map/convert_element_type | solution.py:414
  19.4 2.9 %collective-permute-start.1 = (bf16[4,384,256]{2,1,0:T(8,128)(2,1)}, bf16[4,384,256]{2,1,0:T(8,128)(2,1)}, u32[]{:S(2)}, u32[]{:S(2)}) collective-permute-start(bf16[4,384,256]{2,1,0:T(8,128)(2,1)} %get-tuple-element.22), channel_id=1, source_target_pairs={{0,4},{2,6},{4,0},{6,2},{8,12},{10,14},{12,8},{14,10},{16,20},{18,... | collective-permute-start | bytes 2359304 | tf_op jit(solution)/shard_map/ppermute | solution.py:402
  22.3 1.6 %collective-permute-start.6 = (bf16[384,256]{1,0:T(8,128)(2,1)S(1)}, bf16[384,256]{1,0:T(8,128)(2,1)S(1)}, u32[]{:S(2)}, u32[]{:S(2)}) collective-permute-start(bf16[384,256]{1,0:T(8,128)(2,1)S(1)} %get-tuple-element.23), channel_id=1, source_target_pairs={{0,8},{2,10},{4,12},{6,14},{8,16},{10,18},{12,20},{14,22},{16,24},... | collective-permute-start | bytes 589832 | tf_op jit(solution)/shard_map/ppermute | solution.py:402
  23.9 2.6 %collective-permute-start.7 = (bf16[384,256]{1,0:T(8,128)(2,1)S(1)}, bf16[384,256]{1,0:T(8,128)(2,1)S(1)}, u32[]{:S(2)}, u32[]{:S(2)}) collective-permute-start(bf16[384,256]{1,0:T(8,128)(2,1)S(1)} %get-tuple-element.25), channel_id=1, source_target_pairs={{0,16},{2,18},{4,20},{6,22},{8,24},{10,26},{12,28},{14,30},{16,0},... | collective-permute-start | bytes 589832 | tf_op jit(solution)/shard_map/ppermute | solution.py:402
  26.5 1.4 collective-permute-start.8
  27.9 12.5 %collective-permute-done.1 = bf16[4,384,256]{2,1,0:T(8,128)(2,1)} collective-permute-done((bf16[4,384,256]{2,1,0:T(8,128)(2,1)}, bf16[4,384,256]{2,1,0:T(8,128)(2,1)}, u32[]{:S(2)}, u32[]{:S(2)}) %collective-permute-start.1) | collective-permute-done | bytes 786464 | tf_op jit(solution)/shard_map/ppermute | solution.py:402
  40.4 1.7 %add_convert_fusion.1 = bf16[4,384,256]{2,1,0:T(8,128)(2,1)S(1)} fusion(bf16[4,384,256]{2,1,0:T(8,128)(2,1)} %collective-permute-done.1, bf16[4,1152,256]{2,1,0:T(8,128)(2,1)S(1)} %collective-permute-done, s32[]{:T(128)S(6)} %select_n.114, bf16[4,1152,256]{2,1,0:T(8,128)(2,1)} %get-tuple-element.13), kind=kLoop, calls=%fused_computation.1 | loop fusion | flops 2359296 | bytes 3145732 | tf_op jit(solution)/shard_map/convert_element_type | solution.py:448
  42.1 1.9 %collective-permute-start.2 = (bf16[384,256]{1,0:T(8,128)(2,1)S(1)}, bf16[384,256]{1,0:T(8,128)(2,1)S(1)}, u32[]{:S(2)}, u32[]{:S(2)}) collective-permute-start(bf16[384,256]{1,0:T(8,128)(2,1)S(1)} %get-tuple-element.26), channel_id=1, source_target_pairs={{0,8},{2,10},{4,12},{6,14},{8,16},{10,18},{12,20},{14,22},{16,24},... | collective-permute-start | bytes 589832 | tf_op jit(solution)/shard_map/ppermute | solution.py:402
  44.0 2.6 %collective-permute-start.3 = (bf16[384,256]{1,0:T(8,128)(2,1)S(1)}, bf16[384,256]{1,0:T(8,128)(2,1)S(1)}, u32[]{:S(2)}, u32[]{:S(2)}) collective-permute-start(bf16[384,256]{1,0:T(8,128)(2,1)S(1)} %get-tuple-element.28), channel_id=1, source_target_pairs={{0,16},{2,18},{4,20},{6,22},{8,24},{10,26},{12,28},{14,30},{16,0},... | collective-permute-start | bytes 589832 | tf_op jit(solution)/shard_map/ppermute | solution.py:402
  46.6 1.3 collective-permute-start.4
  48.0 1.6 collective-permute-start.9
  49.6 2.2 %collective-permute-done.2 = bf16[384,256]{1,0:T(8,128)(2,1)S(1)} collective-permute-done((bf16[384,256]{1,0:T(8,128)(2,1)S(1)}, bf16[384,256]{1,0:T(8,128)(2,1)S(1)}, u32[]{:S(2)}, u32[]{:S(2)}) %collective-permute-start.2) | collective-permute-done | bytes 196640 | tf_op jit(solution)/shard_map/ppermute | solution.py:402
  51.9 7.0 %collective-permute-done.3 = bf16[384,256]{1,0:T(8,128)(2,1)S(1)} collective-permute-done((bf16[384,256]{1,0:T(8,128)(2,1)S(1)}, bf16[384,256]{1,0:T(8,128)(2,1)S(1)}, u32[]{:S(2)}, u32[]{:S(2)}) %collective-permute-start.3) | collective-permute-done | bytes 196640 | tf_op jit(solution)/shard_map/ppermute | solution.py:402
  59.0 1.6 collective-permute-start.5
  60.7 0.5 collective-permute-start.10
  61.2 4.6 %collective-permute-done.5.refs_3_ = bf16[384,256]{1,0:T(8,128)(2,1)S(1)} collective-permute-done((bf16[384,256]{1,0:T(8,128)(2,1)S(1)}, bf16[384,256]{1,0:T(8,128)(2,1)S(1)}, u32[]{:S(2)}, u32[]{:S(2)}) %collective-permute-start.5) | collective-permute-done | bytes 196640 | tf_op jit(solution)/shard_map/ppermute | solution.py:402
  65.9 1.4 collective-permute-done.11.refs_6_
  67.3 0.6 copy-done.17
  67.9 2.8 %assemble.1 = (bf16[2304,256]{1,0:T(8,128)(2,1)}, f32[8,128]{1,0:T(8,128)}) custom-call(s32[17]{0:T(128)} %stack.67.info.refs_0_, f32[1]{0:T(128)} %bitcast.17.refs_1_.refs_0_, bf16[384,256]{1,0:T(8,128)(2,1)} %copy-done, bf16[384,256]{1,0:T(8,128)(2,1)} %copy-done.14, bf16[384,256]{1,0:T(8,128)(2,1)} %copy-done.1, bf16[384,256]{1,0:T(8,128)(2,1)} %copy-done.16, ...), custom_call_target="tpu_custom_call" | custom-call | tf_op jit(solution)/shard_map/assemble/pallas_call | solution.py:376
  70.7 4.8 %collective-permute-start.13 = (f32[8,128]{1,0:T(8,128)}, f32[8,128]{1,0:T(8,128)S(1)}, u32[]{:S(2)}, u32[]{:S(2)}) collective-permute-start(f32[8,128]{1,0:T(8,128)} %get-tuple-element.15), channel_id=1, source_target_pairs={{0,8},{2,10},{4,12},{6,14},{8,16},{10,18},{12,20},{14,22},{16,24},... | collective-permute-start | bytes 12296 | tf_op jit(solution)/shard_map/ppermute | solution.py:402
  75.5 0.5 collective-permute-start.14
  75.9 1.9 %collective-permute-start.15 = (f32[8,128]{1,0:T(8,128)}, f32[8,128]{1,0:T(8,128)S(1)}, u32[]{:S(2)}, u32[]{:S(2)}) collective-permute-start(f32[8,128]{1,0:T(8,128)} %get-tuple-element.15), channel_id=1, source_target_pairs={{0,24},{2,26},{4,28},{6,30},{8,0},{10,2},{12,4},{14,6},{16,8},{18,... | collective-permute-start | bytes 12296 | tf_op jit(solution)/shard_map/ppermute | solution.py:402
  77.8 2.3 %collective-permute-done.14 = f32[8,128]{1,0:T(8,128)S(1)} collective-permute-done((f32[8,128]{1,0:T(8,128)}, f32[8,128]{1,0:T(8,128)S(1)}, u32[]{:S(2)}, u32[]{:S(2)}) %collective-permute-start.14) | collective-permute-done | bytes 4128 | tf_op jit(solution)/shard_map/ppermute | solution.py:402
  80.2 0.7 maximum_maximum_fusion
  80.9 1.5 collective-permute-start.16
  82.3 7.3 %powers.1 = (bf16[1024,1024]{1,0:T(8,128)(2,1)}, bf16[1024,1024]{1,0:T(8,128)(2,1)}) custom-call(f32[1]{0:T(128)} %bitcast.17.refs_1_.refs_0_, bf16[2304,256]{1,0:T(8,128)(2,1)} %get-tuple-element.16.refs_1_.refs_3_), custom_call_target="tpu_custom_call" | custom-call | flops 4294967296 | bytes 6291456 | tf_op jit(solution)/shard_map/powers/pallas_call | solution.py:193
  89.7 0.6 max.15.refs_2_
  90.3 12.0 %finish.1 = (bf16[2304,256]{1,0:T(8,128)(2,1)}, bf16[576,256]{1,0:T(8,128)(2,1)}) custom-call(s32[17]{0:T(128)} %stack.67.info.refs_0_, f32[1]{0:T(128)} %bitcast.17.refs_1_.refs_0_, f32[8,128]{1,0:T(8,128)} %max.15.refs_2_, bf16[2304,256]{1,0:T(8,128)(2,1)} %get-tuple-element.16.refs_1_.refs_3_, bf16[1024,1024]{1,0:T(8,128)(2,1)} %get-tuple-element.17.refs_4_, ...), custom_call_target="tpu_custom_call" | custom-call | tf_op jit(solution)/shard_map/finish/pallas_call | solution.py:244
  102.3 3.3 %collective-permute-start.25 = (bf16[576,256]{1,0:T(8,128)(2,1)}, bf16[576,256]{1,0:T(8,128)(2,1)S(1)}, u32[]{:S(2)}, u32[]{:S(2)}) collective-permute-start(bf16[576,256]{1,0:T(8,128)(2,1)} %get-tuple-element.19), channel_id=1, source_target_pairs={{0,24},{2,26},{4,28},{6,30},{8,0},{10,2},{12,4},{14,6},{16,8},{18,... | collective-permute-start | bytes 884744 | tf_op jit(solution)/shard_map/ppermute | solution.py:402
  105.6 7.7 %collective-permute-done.25.refs_1_ = bf16[576,256]{1,0:T(8,128)(2,1)S(1)} collective-permute-done((bf16[576,256]{1,0:T(8,128)(2,1)}, bf16[576,256]{1,0:T(8,128)(2,1)S(1)}, u32[]{:S(2)}, u32[]{:S(2)}) %collective-permute-start.25) | collective-permute-done | bytes 294944 | tf_op jit(solution)/shard_map/ppermute | solution.py:402
  113.3 1.5 collective-permute-start.26
  114.8 2.9 %collective-permute-done.17.refs_1_ = bf16[576,256]{1,0:T(8,128)(2,1)S(1)} collective-permute-done((bf16[576,256]{1,0:T(8,128)(2,1)}, bf16[576,256]{1,0:T(8,128)(2,1)S(1)}, u32[]{:S(2)}, u32[]{:S(2)}) %collective-permute-start.17) | collective-permute-done | bytes 294944 | tf_op jit(solution)/shard_map/ppermute | solution.py:402
  117.7 1.8 %collective-permute-start.21 = (bf16[576,256]{1,0:T(8,128)(2,1)S(1)}, bf16[576,256]{1,0:T(8,128)(2,1)S(1)}, u32[]{:S(2)}, u32[]{:S(2)}) collective-permute-start(bf16[576,256]{1,0:T(8,128)(2,1)S(1)} %collective-permute-done.17.refs_1_), channel_id=1, source_target_pairs={{0,8},{2,10},{4,12},{6,14},{8,16},{10,18},{12,20},{14,22},{16,24},... | collective-permute-start | bytes 884744 | tf_op jit(solution)/shard_map/ppermute | solution.py:402
  119.5 1.5 collective-permute-start.18
  121.3 5.0 %collective-permute-done.21.refs_5_ = bf16[576,256]{1,0:T(8,128)(2,1)S(1)} collective-permute-done((bf16[576,256]{1,0:T(8,128)(2,1)S(1)}, bf16[576,256]{1,0:T(8,128)(2,1)S(1)}, u32[]{:S(2)}, u32[]{:S(2)}) %collective-permute-start.21) | collective-permute-done | bytes 294944 | tf_op jit(solution)/shard_map/ppermute | solution.py:402
  126.2 1.5 collective-permute-start.22
  127.8 8.5 %apply.3.refs_6_ = f32[4096,1792]{1,0:T(8,128)} custom-call(s32[17]{0:T(128)} %stack.67.info.refs_0_, bf16[2304,256]{1,0:T(8,128)(2,1)} %get-tuple-element.20.refs_1_, bf16[2,4096,1792]{2,1,0:T(8,128)(2,1)} %refs_9_.1), custom_call_target="tpu_custom_call" | custom-call | flops 3758096384 | bytes 11010048 | tf_op jit(solution)/shard_map/apply/pallas_call | solution.py:320
  136.4 0.5 collective-permute-start.23
  137.0 0.4 collective-permute-start.24
  137.5 0.7 copy-done.10
  138.2 8.5 %apply.4.refs_10_ = f32[4096,1792]{1,0:T(8,128)} custom-call(s32[17]{0:T(128)} %stack.67.info.refs_0_, bf16[576,256]{1,0:T(8,128)(2,1)} %copy-done.4, bf16[576,256]{1,0:T(8,128)(2,1)} %copy-done.6, bf16[576,256]{1,0:T(8,128)(2,1)} %copy-done.8, bf16[576,256]{1,0:T(8,128)(2,1)} %copy-done.10, ...), custom_call_target="tpu_custom_call", output_to_operand_aliasing={{}: (6, {})} | custom-call | flops 3758096384 | bytes 11010048 | tf_op jit(solution)/shard_map/apply/pallas_call | solution.py:320
  146.8 0.7 copy-done.9
  147.6 0.7 copy-done.13
  148.4 12.9 %apply.5 = f32[4096,1792]{1,0:T(8,128)} custom-call(s32[17]{0:T(128)} %stack.67.info.refs_0_, bf16[576,256]{1,0:T(8,128)(2,1)} %copy-done.2, bf16[576,256]{1,0:T(8,128)(2,1)} %copy-done.5, bf16[576,256]{1,0:T(8,128)(2,1)} %copy-done.9, bf16[576,256]{1,0:T(8,128)(2,1)} %copy-done.12, bf16[576,256]{1,0:T(8,128)(2,1)} %copy-done.3, ...), custom_call_target="tpu_custom_call", output_to_operand_aliasing={{}: (10, {})} | custom-call | flops 7516192768 | bytes 22020096 | tf_op jit(solution)/shard_map/apply/pallas_call | solution.py:320
  (63 shorter events, 1.1 us)
Async XLA Ops:
  11.9 4.9 %collective-permute-start = (bf16[4,1152,256]{2,1,0:T(8,128)(2,1)}, bf16[4,1152,256]{2,1,0:T(8,128)(2,1)S(1)}, u32[]{:S(2)}, u32[]{:S(2)}) collective-permute-start(bf16[4,1152,256]{2,1,0:T(8,128)(2,1)} %get-tuple-element.14), channel_id=1, source_target_pairs={{0,2},{2,0},{4,6},{6,4},{8,10},{10,8},{12,14},{14,12},{16,18},{18,... | collective-permute-start | bytes 7077896 | tf_op jit(solution)/shard_map/ppermute | solution.py:402
  19.4 21.0 %collective-permute-start.1 = (bf16[4,384,256]{2,1,0:T(8,128)(2,1)}, bf16[4,384,256]{2,1,0:T(8,128)(2,1)}, u32[]{:S(2)}, u32[]{:S(2)}) collective-permute-start(bf16[4,384,256]{2,1,0:T(8,128)(2,1)} %get-tuple-element.22), channel_id=1, source_target_pairs={{0,4},{2,6},{4,0},{6,2},{8,12},{10,14},{12,8},{14,10},{16,20},{18,... | collective-permute-start | bytes 2359304 | tf_op jit(solution)/shard_map/ppermute | solution.py:402
  22.3 24.3 %collective-permute-start.6 = (bf16[384,256]{1,0:T(8,128)(2,1)S(1)}, bf16[384,256]{1,0:T(8,128)(2,1)S(1)}, u32[]{:S(2)}, u32[]{:S(2)}) collective-permute-start(bf16[384,256]{1,0:T(8,128)(2,1)S(1)} %get-tuple-element.23), channel_id=1, source_target_pairs={{0,8},{2,10},{4,12},{6,14},{8,16},{10,18},{12,20},{14,22},{16,24},... | collective-permute-start | bytes 589832 | tf_op jit(solution)/shard_map/ppermute | solution.py:402
  23.9 24.0 %collective-permute-start.7 = (bf16[384,256]{1,0:T(8,128)(2,1)S(1)}, bf16[384,256]{1,0:T(8,128)(2,1)S(1)}, u32[]{:S(2)}, u32[]{:S(2)}) collective-permute-start(bf16[384,256]{1,0:T(8,128)(2,1)S(1)} %get-tuple-element.25), channel_id=1, source_target_pairs={{0,16},{2,18},{4,20},{6,22},{8,24},{10,26},{12,28},{14,30},{16,0},... | collective-permute-start | bytes 589832 | tf_op jit(solution)/shard_map/ppermute | solution.py:402
  26.5 21.4 %collective-permute-start.8 = (bf16[384,256]{1,0:T(8,128)(2,1)S(1)}, bf16[384,256]{1,0:T(8,128)(2,1)S(1)}, u32[]{:S(2)}, u32[]{:S(2)}) collective-permute-start(bf16[384,256]{1,0:T(8,128)(2,1)S(1)} %get-tuple-element.24), channel_id=1, source_target_pairs={{0,24},{2,26},{4,28},{6,30},{8,0},{10,2},{12,4},{14,6},{16,8},{18,... | collective-permute-start | bytes 589832 | tf_op jit(solution)/shard_map/ppermute | solution.py:402
  42.1 9.7 %collective-permute-start.2 = (bf16[384,256]{1,0:T(8,128)(2,1)S(1)}, bf16[384,256]{1,0:T(8,128)(2,1)S(1)}, u32[]{:S(2)}, u32[]{:S(2)}) collective-permute-start(bf16[384,256]{1,0:T(8,128)(2,1)S(1)} %get-tuple-element.26), channel_id=1, source_target_pairs={{0,8},{2,10},{4,12},{6,14},{8,16},{10,18},{12,20},{14,22},{16,24},... | collective-permute-start | bytes 589832 | tf_op jit(solution)/shard_map/ppermute | solution.py:402
  44.0 14.9 %collective-permute-start.3 = (bf16[384,256]{1,0:T(8,128)(2,1)S(1)}, bf16[384,256]{1,0:T(8,128)(2,1)S(1)}, u32[]{:S(2)}, u32[]{:S(2)}) collective-permute-start(bf16[384,256]{1,0:T(8,128)(2,1)S(1)} %get-tuple-element.28), channel_id=1, source_target_pairs={{0,16},{2,18},{4,20},{6,22},{8,24},{10,26},{12,28},{14,30},{16,0},... | collective-permute-start | bytes 589832 | tf_op jit(solution)/shard_map/ppermute | solution.py:402
  46.6 12.3 %collective-permute-start.4 = (bf16[384,256]{1,0:T(8,128)(2,1)S(1)}, bf16[384,256]{1,0:T(8,128)(2,1)S(1)}, u32[]{:S(2)}, u32[]{:S(2)}) collective-permute-start(bf16[384,256]{1,0:T(8,128)(2,1)S(1)} %get-tuple-element.27), channel_id=1, source_target_pairs={{0,24},{2,26},{4,28},{6,30},{8,0},{10,2},{12,4},{14,6},{16,8},{18,... | collective-permute-start | bytes 589832 | tf_op jit(solution)/shard_map/ppermute | solution.py:402
  48.0 12.6 %collective-permute-start.9 = (bf16[384,256]{1,0:T(8,128)(2,1)S(1)}, bf16[384,256]{1,0:T(8,128)(2,1)S(1)}, u32[]{:S(2)}, u32[]{:S(2)}) collective-permute-start(bf16[384,256]{1,0:T(8,128)(2,1)S(1)} %fusion.2), channel_id=1, source_target_pairs={{0,4},{2,6},{4,0},{6,2},{8,12},{10,14},{12,8},{14,10},{16,20},{18,... | collective-permute-start | bytes 589832 | tf_op jit(solution)/shard_map/ppermute | solution.py:402
  59.0 8.3 %copy-start = (bf16[384,256]{1,0:T(8,128)(2,1)}, bf16[384,256]{1,0:T(8,128)(2,1)S(1)}, u32[]{:S(2)}) copy-start(bf16[384,256]{1,0:T(8,128)(2,1)S(1)} %fusion.5.refs_2_) | copy-start | bytes 589828
  59.0 6.8 %collective-permute-start.5 = (bf16[384,256]{1,0:T(8,128)(2,1)S(1)}, bf16[384,256]{1,0:T(8,128)(2,1)S(1)}, u32[]{:S(2)}, u32[]{:S(2)}) collective-permute-start(bf16[384,256]{1,0:T(8,128)(2,1)S(1)} %fusion.5.refs_2_), channel_id=1, source_target_pairs={{0,4},{2,6},{4,0},{6,2},{8,12},{10,14},{12,8},{14,10},{16,20},{18,... | collective-permute-start | bytes 589832 | tf_op jit(solution)/shard_map/ppermute | solution.py:402
  60.6 6.6 %copy-start.1 = (bf16[384,256]{1,0:T(8,128)(2,1)}, bf16[384,256]{1,0:T(8,128)(2,1)S(1)}, u32[]{:S(2)}) copy-start(bf16[384,256]{1,0:T(8,128)(2,1)S(1)} %add_convert_fusion.3.refs_4_) | copy-start | bytes 589828
  60.7 5.2 %collective-permute-start.12 = (bf16[384,256]{1,0:T(8,128)(2,1)S(1)}, bf16[384,256]{1,0:T(8,128)(2,1)S(1)}, u32[]{:S(2)}, u32[]{:S(2)}) collective-permute-start(bf16[384,256]{1,0:T(8,128)(2,1)S(1)} %add_convert_fusion.3.refs_4_), channel_id=1, source_target_pairs={{0,2},{2,0},{4,6},{6,4},{8,10},{10,8},{12,14},{14,12},{16,18},{18,... | collective-permute-start | bytes 589832 | tf_op jit(solution)/shard_map/ppermute | solution.py:402
  60.7 5.1 %collective-permute-start.10 = (bf16[384,256]{1,0:T(8,128)(2,1)S(1)}, bf16[384,256]{1,0:T(8,128)(2,1)S(1)}, u32[]{:S(2)}, u32[]{:S(2)}) collective-permute-start(bf16[384,256]{1,0:T(8,128)(2,1)S(1)} %fusion.5.refs_2_), channel_id=1, source_target_pairs={{0,2},{2,0},{4,6},{6,4},{8,10},{10,8},{12,14},{14,12},{16,18},{18,... | collective-permute-start | bytes 589832 | tf_op jit(solution)/shard_map/ppermute | solution.py:402
  65.8 1.5 copy-start.14
  65.8 1.4 collective-permute-start.11
  65.8 1.4 copy-start.15
  65.8 1.4 copy-start.16
  67.3 0.7 copy-start.17
  70.7 7.1 %collective-permute-start.13 = (f32[8,128]{1,0:T(8,128)}, f32[8,128]{1,0:T(8,128)S(1)}, u32[]{:S(2)}, u32[]{:S(2)}) collective-permute-start(f32[8,128]{1,0:T(8,128)} %get-tuple-element.15), channel_id=1, source_target_pairs={{0,8},{2,10},{4,12},{6,14},{8,16},{10,18},{12,20},{14,22},{16,24},... | collective-permute-start | bytes 12296 | tf_op jit(solution)/shard_map/ppermute | solution.py:402
  75.5 4.7 %collective-permute-start.14 = (f32[8,128]{1,0:T(8,128)}, f32[8,128]{1,0:T(8,128)S(1)}, u32[]{:S(2)}, u32[]{:S(2)}) collective-permute-start(f32[8,128]{1,0:T(8,128)} %get-tuple-element.15), channel_id=1, source_target_pairs={{0,16},{2,18},{4,20},{6,22},{8,24},{10,26},{12,28},{14,30},{16,0},... | collective-permute-start | bytes 12296 | tf_op jit(solution)/shard_map/ppermute | solution.py:402
  75.9 4.3 %collective-permute-start.15 = (f32[8,128]{1,0:T(8,128)}, f32[8,128]{1,0:T(8,128)S(1)}, u32[]{:S(2)}, u32[]{:S(2)}) collective-permute-start(f32[8,128]{1,0:T(8,128)} %get-tuple-element.15), channel_id=1, source_target_pairs={{0,24},{2,26},{4,28},{6,30},{8,0},{10,2},{12,4},{14,6},{16,8},{18,... | collective-permute-start | bytes 12296 | tf_op jit(solution)/shard_map/ppermute | solution.py:402
  80.9 8.8 %collective-permute-start.16 = (f32[8,128]{1,0:T(8,128)S(1)}, f32[8,128]{1,0:T(8,128)S(1)}, u32[]{:S(2)}, u32[]{:S(2)}) collective-permute-start(f32[8,128]{1,0:T(8,128)S(1)} %maximum_maximum_fusion), channel_id=1, source_target_pairs={{0,1},{1,0},{2,3},{3,2},{4,5},{5,4},{6,7},{7,6},{8,9},{9,8},{10,11... | collective-permute-start | bytes 12296 | tf_op jit(solution)/shard_map/ppermute | solution.py:464
  102.3 11.0 %collective-permute-start.25 = (bf16[576,256]{1,0:T(8,128)(2,1)}, bf16[576,256]{1,0:T(8,128)(2,1)S(1)}, u32[]{:S(2)}, u32[]{:S(2)}) collective-permute-start(bf16[576,256]{1,0:T(8,128)(2,1)} %get-tuple-element.19), channel_id=1, source_target_pairs={{0,24},{2,26},{4,28},{6,30},{8,0},{10,2},{12,4},{14,6},{16,8},{18,... | collective-permute-start | bytes 884744 | tf_op jit(solution)/shard_map/ppermute | solution.py:402
  105.6 12.1 %collective-permute-start.17 = (bf16[576,256]{1,0:T(8,128)(2,1)}, bf16[576,256]{1,0:T(8,128)(2,1)S(1)}, u32[]{:S(2)}, u32[]{:S(2)}) collective-permute-start(bf16[576,256]{1,0:T(8,128)(2,1)} %get-tuple-element.19), channel_id=1, source_target_pairs={{0,8},{2,10},{4,12},{6,14},{8,16},{10,18},{12,20},{14,22},{16,24},... | collective-permute-start | bytes 884744 | tf_op jit(solution)/shard_map/ppermute | solution.py:402
  113.3 23.0 %copy-start.4 = (bf16[576,256]{1,0:T(8,128)(2,1)}, bf16[576,256]{1,0:T(8,128)(2,1)S(1)}, u32[]{:S(2)}) copy-start(bf16[576,256]{1,0:T(8,128)(2,1)S(1)} %collective-permute-done.25.refs_1_) | copy-start | bytes 884740
  113.3 7.7 %collective-permute-start.26 = (bf16[576,256]{1,0:T(8,128)(2,1)S(1)}, bf16[576,256]{1,0:T(8,128)(2,1)S(1)}, u32[]{:S(2)}, u32[]{:S(2)}) collective-permute-start(bf16[576,256]{1,0:T(8,128)(2,1)S(1)} %collective-permute-done.25.refs_1_), channel_id=1, source_target_pairs={{0,4},{2,6},{4,0},{6,2},{8,12},{10,14},{12,8},{14,10},{16,20},{18,... | collective-permute-start | bytes 884744 | tf_op jit(solution)/shard_map/ppermute | solution.py:402
  117.7 18.6 %copy-start.2 = (bf16[576,256]{1,0:T(8,128)(2,1)}, bf16[576,256]{1,0:T(8,128)(2,1)S(1)}, u32[]{:S(2)}) copy-start(bf16[576,256]{1,0:T(8,128)(2,1)S(1)} %collective-permute-done.17.refs_1_) | copy-start | bytes 884740
  117.7 8.5 %collective-permute-start.21 = (bf16[576,256]{1,0:T(8,128)(2,1)S(1)}, bf16[576,256]{1,0:T(8,128)(2,1)S(1)}, u32[]{:S(2)}, u32[]{:S(2)}) collective-permute-start(bf16[576,256]{1,0:T(8,128)(2,1)S(1)} %collective-permute-done.17.refs_1_), channel_id=1, source_target_pairs={{0,8},{2,10},{4,12},{6,14},{8,16},{10,18},{12,20},{14,22},{16,24},... | collective-permute-start | bytes 884744 | tf_op jit(solution)/shard_map/ppermute | solution.py:402
  119.5 16.9 %collective-permute-start.27 = (bf16[576,256]{1,0:T(8,128)(2,1)S(1)}, bf16[576,256]{1,0:T(8,128)(2,1)S(1)}, u32[]{:S(2)}, u32[]{:S(2)}) collective-permute-start(bf16[576,256]{1,0:T(8,128)(2,1)S(1)} %collective-permute-done.25.refs_1_), channel_id=1, source_target_pairs={{0,2},{2,0},{4,6},{6,4},{8,10},{10,8},{12,14},{14,12},{16,18},{18,... | collective-permute-start | bytes 884744 | tf_op jit(solution)/shard_map/ppermute | solution.py:402
  119.5 17.4 %collective-permute-start.18 = (bf16[576,256]{1,0:T(8,128)(2,1)S(1)}, bf16[576,256]{1,0:T(8,128)(2,1)S(1)}, u32[]{:S(2)}, u32[]{:S(2)}) collective-permute-start(bf16[576,256]{1,0:T(8,128)(2,1)S(1)} %collective-permute-done.17.refs_1_), channel_id=1, source_target_pairs={{0,4},{2,6},{4,0},{6,2},{8,12},{10,14},{12,8},{14,10},{16,20},{18,... | collective-permute-start | bytes 884744 | tf_op jit(solution)/shard_map/ppermute | solution.py:402
  121.0 15.2 %copy-start.6 = (bf16[576,256]{1,0:T(8,128)(2,1)}, bf16[576,256]{1,0:T(8,128)(2,1)S(1)}, u32[]{:S(2)}) copy-start(bf16[576,256]{1,0:T(8,128)(2,1)S(1)} %collective-permute-done.26.refs_2_) | copy-start | bytes 884740
  121.0 16.4 %collective-permute-start.28 = (bf16[576,256]{1,0:T(8,128)(2,1)S(1)}, bf16[576,256]{1,0:T(8,128)(2,1)S(1)}, u32[]{:S(2)}, u32[]{:S(2)}) collective-permute-start(bf16[576,256]{1,0:T(8,128)(2,1)S(1)} %collective-permute-done.26.refs_2_), channel_id=1, source_target_pairs={{0,2},{2,0},{4,6},{6,4},{8,10},{10,8},{12,14},{14,12},{16,18},{18,... | collective-permute-start | bytes 884744 | tf_op jit(solution)/shard_map/ppermute | solution.py:402
  126.2 10.1 %copy-start.3 = (bf16[576,256]{1,0:T(8,128)(2,1)}, bf16[576,256]{1,0:T(8,128)(2,1)S(1)}, u32[]{:S(2)}) copy-start(bf16[576,256]{1,0:T(8,128)(2,1)S(1)} %collective-permute-done.21.refs_5_) | copy-start | bytes 884740
  126.2 10.8 %collective-permute-start.22 = (bf16[576,256]{1,0:T(8,128)(2,1)S(1)}, bf16[576,256]{1,0:T(8,128)(2,1)S(1)}, u32[]{:S(2)}, u32[]{:S(2)}) collective-permute-start(bf16[576,256]{1,0:T(8,128)(2,1)S(1)} %collective-permute-done.21.refs_5_), channel_id=1, source_target_pairs={{0,4},{2,6},{4,0},{6,2},{8,12},{10,14},{12,8},{14,10},{16,20},{18,... | collective-permute-start | bytes 884744 | tf_op jit(solution)/shard_map/ppermute | solution.py:402
  136.3 10.4 %collective-permute-start.19 = (bf16[576,256]{1,0:T(8,128)(2,1)S(1)}, bf16[576,256]{1,0:T(8,128)(2,1)S(1)}, u32[]{:S(2)}, u32[]{:S(2)}) collective-permute-start(bf16[576,256]{1,0:T(8,128)(2,1)S(1)} %collective-permute-done.17.refs_1_), channel_id=1, source_target_pairs={{0,2},{2,0},{4,6},{6,4},{8,10},{10,8},{12,14},{14,12},{16,18},{18,... | collective-permute-start | bytes 884744 | tf_op jit(solution)/shard_map/ppermute | solution.py:402
  136.4 1.1 copy-start.8
  136.4 10.3 %collective-permute-start.23 = (bf16[576,256]{1,0:T(8,128)(2,1)S(1)}, bf16[576,256]{1,0:T(8,128)(2,1)S(1)}, u32[]{:S(2)}, u32[]{:S(2)}) collective-permute-start(bf16[576,256]{1,0:T(8,128)(2,1)S(1)} %collective-permute-done.21.refs_5_), channel_id=1, source_target_pairs={{0,2},{2,0},{4,6},{6,4},{8,10},{10,8},{12,14},{14,12},{16,18},{18,... | collective-permute-start | bytes 884744 | tf_op jit(solution)/shard_map/ppermute | solution.py:402
  136.9 9.7 %copy-start.5 = (bf16[576,256]{1,0:T(8,128)(2,1)}, bf16[576,256]{1,0:T(8,128)(2,1)S(1)}, u32[]{:S(2)}) copy-start(bf16[576,256]{1,0:T(8,128)(2,1)S(1)} %collective-permute-done.18.refs_2_) | copy-start | bytes 884740
  136.9 9.8 %collective-permute-start.20 = (bf16[576,256]{1,0:T(8,128)(2,1)S(1)}, bf16[576,256]{1,0:T(8,128)(2,1)S(1)}, u32[]{:S(2)}, u32[]{:S(2)}) collective-permute-start(bf16[576,256]{1,0:T(8,128)(2,1)S(1)} %collective-permute-done.18.refs_2_), channel_id=1, source_target_pairs={{0,2},{2,0},{4,6},{6,4},{8,10},{10,8},{12,14},{14,12},{16,18},{18,... | collective-permute-start | bytes 884744 | tf_op jit(solution)/shard_map/ppermute | solution.py:402
  137.0 9.6 %copy-start.7 = (bf16[576,256]{1,0:T(8,128)(2,1)}, bf16[576,256]{1,0:T(8,128)(2,1)S(1)}, u32[]{:S(2)}) copy-start(bf16[576,256]{1,0:T(8,128)(2,1)S(1)} %collective-permute-done.22.refs_6_) | copy-start | bytes 884740
  137.0 9.7 %collective-permute-start.24 = (bf16[576,256]{1,0:T(8,128)(2,1)S(1)}, bf16[576,256]{1,0:T(8,128)(2,1)S(1)}, u32[]{:S(2)}, u32[]{:S(2)}) collective-permute-start(bf16[576,256]{1,0:T(8,128)(2,1)S(1)} %collective-permute-done.22.refs_6_), channel_id=1, source_target_pairs={{0,2},{2,0},{4,6},{6,4},{8,10},{10,8},{12,14},{14,12},{16,18},{18,... | collective-permute-start | bytes 884744 | tf_op jit(solution)/shard_map/ppermute | solution.py:402
  137.5 0.7 copy-start.10
  146.7 0.7 copy-start.9
  146.7 0.8 copy-start.12
  146.7 0.9 copy-start.11
  147.6 0.7 copy-start.13
